TPU v7x, 16 devices: a whole 2x2x2 slice. The times are simulated.
16 devices in a mesh: dp: 2 (over z), tp: 8 (over y, x, core).
Axes of the slice: x: 2, y: 2, z: 2, core: 2. Of those that a mesh axis runs over, the one named last changes fastest.
Arguments:
- token_ids: int32 [4, 256], P('dp'), parts along dimension 0
- emb_table: bfloat16 [512, 4096], P('tp')
- gain_vec: bfloat16 [4096], replicated
- w_qkv: bfloat16 [4096, 34816], P(None, 'tp')
- grad_u: bfloat16 [4, 256, 34816], P('dp', None, 'tp'), parts along dimension 0
- grad_res: bfloat16 [4, 256, 4096], P('dp', 'tp'), parts along dimension 0
Outputs:
- output 1: bfloat16 [4, 256, 34816], P('dp', None, 'tp'), parts along dimension 0
- output 2: bfloat16 [4, 256, 4096], P('dp', 'tp'), parts along dimension 0
- output 3: float32 [1024, 4096], P(('dp', 'tp')), parts along dimension 0
- output 4: float32 [4096, 69632], P(None, ('dp', 'tp')), parts along dimension 1
- output 5: float32 [8192], P('dp'), parts along dimension 0
There are 2 independent parts. A program takes and returns all parts, laid end to end along the dimension named above; an argument that names none is the same for every part.
All inputs are finite; a program needn't handle non-finite values.
Results may differ from a plain program's by a relative error of at most 0.00497172.
Values are sent between devices in bfloat16 or wider.
A program may use at most 1 GiB of HBM per device.

v0:
```python
import jax
import jax.numpy as jnp
from jax import lax
from jax.sharding import PartitionSpec as P, NamedSharding

NORM_EPS = 1e-6


def solution(mesh):
    group_size = mesh.shape['tp']

    def local_step(token_ids, table_loc, gain_vec, w_loc, du_loc, dres_loc):
        seq_len = token_ids.shape[1]
        rows_loc, model_dim = table_loc.shape
        seq_loc = seq_len // group_size
        cols_loc = w_loc.shape[1]
        dev_idx = lax.axis_index('tp')
        row_start = dev_idx * rows_loc
        tok_start = dev_idx * seq_loc
        gain_f = gain_vec.astype(jnp.float32)

        def micro_step(acc_state, inputs):
            grad_table, grad_w, grad_gain = acc_state
            tok_ids, du_m, dres_m = inputs
            local_ids = tok_ids - row_start
            in_block = (local_ids >= 0) & (local_ids < rows_loc)
            safe_ids = jnp.where(in_block, local_ids, 0)
            looked = jnp.take(table_loc, safe_ids, axis=0)
            partial_x = jnp.where(in_block[:, None], looked, jnp.zeros_like(looked))
            tokens = lax.psum(partial_x, 'tp')
            tok_f = tokens.astype(jnp.float32)
            inv_rms = lax.rsqrt(jnp.mean(tok_f * tok_f, axis=-1, keepdims=True) + NORM_EPS)
            n_hat = tok_f * inv_rms
            normed = (n_hat * gain_f).astype(jnp.bfloat16)
            u_m = jnp.dot(normed, w_loc, preferred_element_type=jnp.float32).astype(jnp.bfloat16)
            x_own = lax.dynamic_slice_in_dim(tokens, tok_start, seq_loc, axis=0)
            dn_part = lax.dot_general(du_m, w_loc, (((1,), (1,)), ((), ())), preferred_element_type=jnp.float32).astype(jnp.bfloat16)
            dn_recv = lax.all_to_all(dn_part.reshape(group_size, seq_loc, model_dim), 'tp', 0, 0, tiled=True)
            d_norm = jnp.sum(dn_recv, axis=0, dtype=jnp.float32)
            hat_own = lax.dynamic_slice_in_dim(n_hat, tok_start, seq_loc, axis=0)
            inv_own = lax.dynamic_slice_in_dim(inv_rms, tok_start, seq_loc, axis=0)
            gain_dn = gain_f * d_norm
            centre = jnp.mean(hat_own * gain_dn, axis=-1, keepdims=True)
            d_x = (dres_m.astype(jnp.float32) + inv_own * (gain_dn - hat_own * centre)).astype(jnp.bfloat16)
            grad_gain = grad_gain + jnp.sum(d_norm * hat_own, axis=0)
            grad_w = grad_w + lax.dot_general(normed, du_m, (((0,), (0,)), ((), ())), preferred_element_type=jnp.float32)
            dx_all = lax.all_gather(d_x, 'tp', axis=0, tiled=True)
            contrib = jnp.where(in_block[:, None], dx_all.astype(jnp.float32), 0.0)
            grad_table = grad_table + jax.ops.segment_sum(contrib, safe_ids, num_segments=rows_loc)
            return (grad_table, grad_w, grad_gain), (u_m, x_own)

        init_state = (jnp.zeros((rows_loc, model_dim), jnp.float32), jnp.zeros((model_dim, cols_loc), jnp.float32), jnp.zeros((model_dim,), jnp.float32))
        (grad_table, grad_w, grad_gain), (u_proj, x_resid) = lax.scan(micro_step, init_state, (token_ids, du_loc, dres_loc))
        grad_gain = lax.psum(grad_gain, 'tp')
        return u_proj, x_resid, grad_table, grad_w, grad_gain

    return jax.shard_map(local_step, mesh=mesh,
                         in_specs=(P('dp', None), P('tp', None), P(None), P(None, 'tp'), P('dp', None, 'tp'), P('dp', 'tp', None)),
                         out_specs=(P('dp', None, 'tp'), P('dp', 'tp', None), P(('dp', 'tp'), None), P(None, ('dp', 'tp')), P('dp')),
                         check_vma=False)
```

profile of v0, /device:TPU:0, one launch (start us, length us, event | category | flops | bytes accessed | tf_op | source)
XLA Modules:
  0.0 329.8 jit_solution(9361278827963158301)
XLA Ops:
  7.2 0.7 convert_element_type.46
  7.9 1.1 broadcast.194
  8.9 291.5 %while.21 = (s32[]{:T(128)}, f32[64,4096]{1,0:T(8,128)}, f32[4096,4352]{1,0:T(8,128)}, f32[4096]{0:T(1024)S(1)}, bf16[2,256,4352]{2,1,0:T(8,128)(2,1)}, /*index=...) while((s32[]{:T(128)}, f32[64,4096]{1,0:T(8,128)}, ...), condition=%wide.region_7.8_spmd.clone, body=%wide.region_0.7_spmd.clone.sunk | while | flops 27441702912 | bytes 301748064 | solution.py:53
  8.9 0.7 compare_select_fusion.3
  9.7 5.0 %gather_fusion = bf16[256,4096]{1,0:T(8,128)(2,1)S(1)} fusion(bf16[64,4096]{1,0:T(8,128)(2,1)} %get-tuple-element.398, s32[1024]{0:T(1024)S(1)} %pad_clamp_fusion.2), kind=kCustom, calls=%fused_computation.clone.clone.1 | custom fusion | bytes 4195328 | tf_op jit(solution)/shard_map/while/body/eval_jaxpr/jit(_take)/gather | solution.py:28
  14.7 1.7 select_select_fusion.2
  16.4 0.0 all-reduce.2.cloned.1.call-update
  16.4 17.7 %convolution_convert_fusion.3 = bf16[256,4096]{1,0:T(8,128)(2,1)} fusion(bf16[4096,4352]{1,0:T(8,128)(2,1)} %get-tuple-element.402, bf16[2,256,4352]{2,1,0:T(8,128)(2,1)} %get-tuple-element.401, s32[]{:T(128)S(6)} %copy.21), kind=kOutput, calls=%fused_computation.8.clone.1 | convolution fusion | flops 9127854080 | bytes 39976964 | tf_op jit(solution)/shard_map/while/body/eval_jaxpr/dot_general | solution.py:37
  34.1 5.5 %all-to-all-start = ((bf16[8,32,4096]{2,1,0:T(8,128)(2,1)}), bf16[8,32,4096]{2,1,0:T(8,128)(2,1)}, u32[]{:S(2)}, u32[]{:S(2)}) async-start(bf16[8,32,4096]{2,1,0:T(8,128)(2,1)} %bitcast.45), calls=%async_computation | async-start | bytes 4194304 | tf_op jit(solution)/shard_map/while/body/eval_jaxpr/all_to_all | solution.py:38
  39.6 0.0 all-gather.2.cloned.1.call-start
  39.6 45.1 %all-reduce.2.cloned.1.call-done = bf16[256,4096]{1,0:T(8,128)(2,1)} async-done(((bf16[256,4096]{1,0:T(8,128)(2,1)}), bf16[256,4096]{1,0:T(8,128)(2,1)}) %all-reduce.2.cloned.1.call-update) | async-done | bytes 2097168 | tf_op jit(solution)/shard_map/while/body/eval_jaxpr/psum | solution.py:30
  84.8 2.1 fusion.35
  86.9 0.1 dynamic-slice.5
  86.9 4.1 %convert_multiply_fusion.5 = f32[256,4096]{1,0:T(8,128)} fusion(bf16[256,4096]{1,0:T(8,128)(2,1)} %all-reduce.2.cloned.1.call-done, f32[256]{0:T(256)S(1)} %add_rsqrt_fusion.2), kind=kLoop, calls=%fused_computation.6.clone.3 | loop fusion | flops 2097152 | bytes 6292480 | tf_op jit(solution)/shard_map/while/body/eval_jaxpr/mul | solution.py:33
  91.1 2.1 convert_reduce_fusion.2
  93.2 1.3 multiply_reduce_fusion.3
  94.4 1.9 fusion.36
  96.4 0.0 all-gather.2.cloned.1.call-update
  96.4 0.0 copy-start.4
  96.4 25.8 %select_add_fusion.4 = f32[4096,4352]{1,0:T(8,128)} fusion(f32[4096,4352]{1,0:T(8,128)} %get-tuple-element.374, pred[]{:T(512)S(6)} %compare.3, bf16[2,256,4352]{2,1,0:T(8,128)(2,1)} %get-tuple-element.401, s32[]{:T(128)S(6)} %copy.21, f32[4096]{0:T(1024)S(1)} %get-tuple-element.400, bf16[256,4096]{1,0:T(8,128)(2,1)S(1)} %copy-done, ...), kind=kOutput, calls=%fused_computation.2.clone.3 | convolution fusion | flops 9166651392 | bytes 146949120 | tf_op jit(solution)/shard_map/while/body/eval_jaxpr/dot_general | solution.py:46
  122.2 0.0 copy-start.5
  122.2 0.8 copy-done.5
  123.0 16.6 %fusion.37 = bf16[2,256,4352]{2,1,0:T(8,128)(2,1)} fusion(bf16[2,256,4352]{2,1,0:T(8,128)(2,1)} %get-tuple-element.376, s32[]{:T(128)S(6)} %copy.21, bf16[4096,4352]{1,0:T(8,128)(2,1)} %get-tuple-element.402, f32[4096]{0:T(1024)S(1)} %get-tuple-element.400, bf16[256,4096]{1,0:T(8,128)(2,1)S(1)} %copy-done, f32[256]{0:T(256)S(1)} %add_rsqrt_fusion.2), kind=kOutput, calls=%fused_computation.5.clone.1 | convolution fusion | flops 9132113920 | bytes 39994372 | tf_op jit(solution)/shard_map/while/body/eval_jaxpr/dot_general | solution.py:35
  139.7 7.7 %scatter_custom_fusion.6 = f32[64,4096]{1,0:T(8,128)S(1)} fusion(f32[64,4096]{1,0:T(8,128)S(1)} %copy-done.2, s32[256]{0:T(256)S(1)} %bitcast.50, bf16[256,4096]{1,0:T(8,128)(2,1)} %all-gather.2.cloned.1.call-done, f32[]{:T(128)} %constant.83.clone.1..sunk, pred[256]{0:T(512)(128)(4,1)S(1)} %get-tuple-element.352), kind=kCustom, calls=%fused_computation.11.clone.1 | custom fusion | flops 3145728 | bytes 3146244 | tf_op jit(solution)/shard_map/while/body/eval_jaxpr/scatter-add | solution.py:49
  147.3 0.0 copy-start.3
  147.4 1.0 copy-done.3
  148.3 0.7 compare_select_fusion.3
  149.0 5.0 %gather_fusion = bf16[256,4096]{1,0:T(8,128)(2,1)S(1)} fusion(bf16[64,4096]{1,0:T(8,128)(2,1)} %get-tuple-element.398, s32[1024]{0:T(1024)S(1)} %pad_clamp_fusion.2), kind=kCustom, calls=%fused_computation.clone.clone.1 | custom fusion | bytes 4195328 | tf_op jit(solution)/shard_map/while/body/eval_jaxpr/jit(_take)/gather | solution.py:28
  154.0 1.7 select_select_fusion.2
  155.7 0.0 all-reduce.2.cloned.1.call-update
  155.8 17.7 %convolution_convert_fusion.3 = bf16[256,4096]{1,0:T(8,128)(2,1)} fusion(bf16[4096,4352]{1,0:T(8,128)(2,1)} %get-tuple-element.402, bf16[2,256,4352]{2,1,0:T(8,128)(2,1)} %get-tuple-element.401, s32[]{:T(128)S(6)} %copy.21), kind=kOutput, calls=%fused_computation.8.clone.1 | convolution fusion | flops 9127854080 | bytes 39976964 | tf_op jit(solution)/shard_map/while/body/eval_jaxpr/dot_general | solution.py:37
  173.5 4.4 %all-to-all-start = ((bf16[8,32,4096]{2,1,0:T(8,128)(2,1)}), bf16[8,32,4096]{2,1,0:T(8,128)(2,1)}, u32[]{:S(2)}, u32[]{:S(2)}) async-start(bf16[8,32,4096]{2,1,0:T(8,128)(2,1)} %bitcast.45), calls=%async_computation | async-start | bytes 4194304 | tf_op jit(solution)/shard_map/while/body/eval_jaxpr/all_to_all | solution.py:38
  177.9 0.0 all-gather.2.cloned.1.call-start
  177.9 38.3 %all-reduce.2.cloned.1.call-done = bf16[256,4096]{1,0:T(8,128)(2,1)} async-done(((bf16[256,4096]{1,0:T(8,128)(2,1)}), bf16[256,4096]{1,0:T(8,128)(2,1)}) %all-reduce.2.cloned.1.call-update) | async-done | bytes 2097168 | tf_op jit(solution)/shard_map/while/body/eval_jaxpr/psum | solution.py:30
  216.2 2.1 fusion.35
  218.3 0.1 dynamic-slice.5
  218.4 4.1 %convert_multiply_fusion.5 = f32[256,4096]{1,0:T(8,128)} fusion(bf16[256,4096]{1,0:T(8,128)(2,1)} %all-reduce.2.cloned.1.call-done, f32[256]{0:T(256)S(1)} %add_rsqrt_fusion.2), kind=kLoop, calls=%fused_computation.6.clone.3 | loop fusion | flops 2097152 | bytes 6292480 | tf_op jit(solution)/shard_map/while/body/eval_jaxpr/mul | solution.py:33
  222.5 2.1 convert_reduce_fusion.2
  224.6 1.3 multiply_reduce_fusion.3
  225.9 1.9 fusion.36
  227.8 0.0 all-gather.2.cloned.1.call-update
  227.8 0.0 copy-start.4
  227.8 46.4 %select_add_fusion.4 = f32[4096,4352]{1,0:T(8,128)} fusion(f32[4096,4352]{1,0:T(8,128)} %get-tuple-element.374, pred[]{:T(512)S(6)} %compare.3, bf16[2,256,4352]{2,1,0:T(8,128)(2,1)} %get-tuple-element.401, s32[]{:T(128)S(6)} %copy.21, f32[4096]{0:T(1024)S(1)} %get-tuple-element.400, bf16[256,4096]{1,0:T(8,128)(2,1)S(1)} %copy-done, ...), kind=kOutput, calls=%fused_computation.2.clone.3 | convolution fusion | flops 9166651392 | bytes 146949120 | tf_op jit(solution)/shard_map/while/body/eval_jaxpr/dot_general | solution.py:46
  274.3 0.8 copy-done.5
  275.1 16.7 %fusion.37 = bf16[2,256,4352]{2,1,0:T(8,128)(2,1)} fusion(bf16[2,256,4352]{2,1,0:T(8,128)(2,1)} %get-tuple-element.376, s32[]{:T(128)S(6)} %copy.21, bf16[4096,4352]{1,0:T(8,128)(2,1)} %get-tuple-element.402, f32[4096]{0:T(1024)S(1)} %get-tuple-element.400, bf16[256,4096]{1,0:T(8,128)(2,1)S(1)} %copy-done, f32[256]{0:T(256)S(1)} %add_rsqrt_fusion.2), kind=kOutput, calls=%fused_computation.5.clone.1 | convolution fusion | flops 9132113920 | bytes 39994372 | tf_op jit(solution)/shard_map/while/body/eval_jaxpr/dot_general | solution.py:35
  291.8 7.7 %scatter_custom_fusion.6 = f32[64,4096]{1,0:T(8,128)S(1)} fusion(f32[64,4096]{1,0:T(8,128)S(1)} %copy-done.2, s32[256]{0:T(256)S(1)} %bitcast.50, bf16[256,4096]{1,0:T(8,128)(2,1)} %all-gather.2.cloned.1.call-done, f32[]{:T(128)} %constant.83.clone.1..sunk, pred[256]{0:T(512)(128)(4,1)S(1)} %get-tuple-element.352), kind=kCustom, calls=%fused_computation.11.clone.1 | custom fusion | flops 3145728 | bytes 3146244 | tf_op jit(solution)/shard_map/while/body/eval_jaxpr/scatter-add | solution.py:49
  299.4 1.0 copy-done.3
  300.4 22.9 %psum.16 = f32[4096]{0:T(1024)} all-reduce(f32[4096]{0:T(1024)S(1)} %get-tuple-element.175), channel_id=1, replica_groups=mesh['dp'=2,'tp'=8] {'tp'}, use_global_device_ids=true, to_apply=%region_8.9 | all-reduce | flops 4096 | bytes 32768 | tf_op jit(solution)/shard_map/psum | solution.py:54
  (38 shorter events, 0.2 us)
Async XLA Ops:
  8.9 75.8 %all-reduce.2.cloned.1.call-start = ((), (), s32[]{:S(2)}) async-start(), calls=%async_computation.1 | async-start | bytes 4194304 | tf_op jit(solution)/shard_map/while/body/eval_jaxpr/psum | solution.py:30
  34.1 57.0 %all-to-all-start = ((bf16[8,32,4096]{2,1,0:T(8,128)(2,1)}), bf16[8,32,4096]{2,1,0:T(8,128)(2,1)}, u32[]{:S(2)}, u32[]{:S(2)}) async-start(bf16[8,32,4096]{2,1,0:T(8,128)(2,1)} %bitcast.45), calls=%async_computation | async-start | bytes 4194304 | tf_op jit(solution)/shard_map/while/body/eval_jaxpr/all_to_all | solution.py:38
  39.6 100.1 %all-gather.2.cloned.1.call-start = ((), (), s32[]{:S(2)}) async-start(), calls=%async_computation.2 | async-start | bytes 2359296 | tf_op jit(solution)/shard_map/while/body/eval_jaxpr/all_gather | solution.py:47
  86.9 7.5 %copy-start.1 = (bf16[2,32,4096]{2,1,0:T(8,128)(2,1)S(1)}, bf16[2,32,4096]{2,1,0:T(8,128)(2,1)}, u32[]{:S(2)}) copy-start(bf16[2,32,4096]{2,1,0:T(8,128)(2,1)} %get-tuple-element.397) | copy-start | bytes 1572868 | tf_op jit(solution)/shard_map/while
  91.1 5.3 %copy-start = (bf16[256,4096]{1,0:T(8,128)(2,1)S(1)}, bf16[256,4096]{1,0:T(8,128)(2,1)}, u32[]{:S(2)}) copy-start(bf16[256,4096]{1,0:T(8,128)(2,1)} %all-reduce.2.cloned.1.call-done) | copy-start | bytes 6291460 | tf_op jit(solution)/shard_map/while
  96.4 25.8 %copy-start.4 = (bf16[2,32,4096]{2,1,0:T(8,128)(2,1)S(1)}, bf16[2,32,4096]{2,1,0:T(8,128)(2,1)}, u32[]{:S(2)}) copy-start(bf16[2,32,4096]{2,1,0:T(8,128)(2,1)} %get-tuple-element.377) | copy-start | bytes 1572868 | tf_op jit(solution)/shard_map/while
  122.2 0.8 copy-start.5
  123.0 16.7 %copy-start.2 = (f32[64,4096]{1,0:T(8,128)S(1)}, f32[64,4096]{1,0:T(8,128)}, u32[]{:S(2)}) copy-start(f32[64,4096]{1,0:T(8,128)} %get-tuple-element.373) | copy-start | bytes 3145732 | tf_op jit(solution)/shard_map/while
  147.3 1.0 copy-start.3
  148.3 67.9 %all-reduce.2.cloned.1.call-start = ((), (), s32[]{:S(2)}) async-start(), calls=%async_computation.1 | async-start | bytes 4194304 | tf_op jit(solution)/shard_map/while/body/eval_jaxpr/psum | solution.py:30
  173.5 49.0 %all-to-all-start = ((bf16[8,32,4096]{2,1,0:T(8,128)(2,1)}), bf16[8,32,4096]{2,1,0:T(8,128)(2,1)}, u32[]{:S(2)}, u32[]{:S(2)}) async-start(bf16[8,32,4096]{2,1,0:T(8,128)(2,1)} %bitcast.45), calls=%async_computation | async-start | bytes 4194304 | tf_op jit(solution)/shard_map/while/body/eval_jaxpr/all_to_all | solution.py:38
  177.9 113.9 %all-gather.2.cloned.1.call-start = ((), (), s32[]{:S(2)}) async-start(), calls=%async_computation.2 | async-start | bytes 2359296 | tf_op jit(solution)/shard_map/while/body/eval_jaxpr/all_gather | solution.py:47
  218.4 7.5 %copy-start.1 = (bf16[2,32,4096]{2,1,0:T(8,128)(2,1)S(1)}, bf16[2,32,4096]{2,1,0:T(8,128)(2,1)}, u32[]{:S(2)}) copy-start(bf16[2,32,4096]{2,1,0:T(8,128)(2,1)} %get-tuple-element.397) | copy-start | bytes 1572868 | tf_op jit(solution)/shard_map/while
  222.5 5.3 %copy-start = (bf16[256,4096]{1,0:T(8,128)(2,1)S(1)}, bf16[256,4096]{1,0:T(8,128)(2,1)}, u32[]{:S(2)}) copy-start(bf16[256,4096]{1,0:T(8,128)(2,1)} %all-reduce.2.cloned.1.call-done) | copy-start | bytes 6291460 | tf_op jit(solution)/shard_map/while
  227.8 46.5 %copy-start.4 = (bf16[2,32,4096]{2,1,0:T(8,128)(2,1)S(1)}, bf16[2,32,4096]{2,1,0:T(8,128)(2,1)}, u32[]{:S(2)}) copy-start(bf16[2,32,4096]{2,1,0:T(8,128)(2,1)} %get-tuple-element.377) | copy-start | bytes 1572868 | tf_op jit(solution)/shard_map/while
  274.3 0.8 copy-start.5
  275.1 16.7 %copy-start.2 = (f32[64,4096]{1,0:T(8,128)S(1)}, f32[64,4096]{1,0:T(8,128)}, u32[]{:S(2)}) copy-start(f32[64,4096]{1,0:T(8,128)} %get-tuple-element.373) | copy-start | bytes 3145732 | tf_op jit(solution)/shard_map/while
  299.4 1.0 copy-start.3
Sparse Core Ops, SparseCore 0:
  16.5 68.2 all-reduce.1
  96.5 23.0 all-gather.1
  155.9 60.2 all-reduce.1
  227.9 23.8 all-gather.1
where the time goes:
time: 331 us; the launch traced here: 330 us
  matrix products  141 us (43%)
  waiting for transfers between devices  83.5 us (25%)
  other arithmetic  43.9 us (13%)
  blocking collectives  22.9 us (7%)
  local copies, waits for them, and re-layouts  14.8 us (4%)
  between operations  13.7 us (4%)
  starting transfers between devices  9.9 us (3%)
    psum x2, waiting for transfers between devices, micro_step(): tokens = lax.psum(partial_x, 'tp')  83.4 us
    dot_general x2, matrix products, micro_step(): lax.dot_general(normed, du_m, (((0,), (0,)), ((), ())), preferred_element...  72.2 us
    dot_general x2, matrix products, micro_step(): lax.dot_general(du_m, w_loc, (((1,), (1,)), ((), ())), preferred_element_...  35.5 us
    dot_general x2, matrix products, micro_step(): jnp.dot(normed, w_loc, preferred_element_type=jnp.float32)  33.3 us
    psum x1, blocking collectives, local_step(): grad_gain = lax.psum(grad_gain, 'tp')  22.9 us
    scatter-add x2, other arithmetic, micro_step(): jax.ops.segment_sum(contrib, safe_ids, num_segments=rows_loc)  15.3 us
    gather x2, local copies, waits for them, and re-layouts, micro_step(): looked = jnp.take(table_loc, safe_ids, axis=0)  9.99 us
    all_to_all x2, starting transfers between devices, micro_step(): lax.all_to_all(dn_part.reshape(group_size, seq_loc, model_dim), 'tp', 0,...  9.81 us
  transfers between devices with their start and end apart: 6, of which 2 were waited for; matrix products, arithmetic and copies ran while one was open for 47% of the time, Pallas kernels for 0%

commit v1 on v0

v1 whole, which is shorter than its diff:
```python
import jax
import jax.numpy as jnp
from jax import lax
from jax.sharding import PartitionSpec as P

NORM_EPS = 1e-6


def solution(mesh):
    group_size = mesh.shape['tp']

    def local_step(token_ids, table_loc, gain_vec, w_loc, du_loc, dres_loc):
        num_micro, seq_len = token_ids.shape
        rows_loc, model_dim = table_loc.shape
        seq_loc = seq_len // group_size
        cols_loc = w_loc.shape[1]
        tokens_all = num_micro * seq_len
        dev_idx = lax.axis_index('tp')
        gain_f = gain_vec.astype(jnp.float32)
        du_flat = du_loc.reshape(tokens_all, cols_loc)

        dn_part = lax.dot_general(du_flat, w_loc, (((1,), (1,)), ((), ())), preferred_element_type=jnp.float32).astype(jnp.bfloat16)
        dn_part = dn_part.reshape(num_micro, group_size, seq_loc, model_dim).transpose(1, 0, 2, 3)
        dn_recv = lax.all_to_all(dn_part, 'tp', 0, 0, tiled=True)
        d_norm = jnp.sum(dn_recv, axis=0, dtype=jnp.float32)

        table = lax.all_gather(table_loc, 'tp', axis=0, tiled=True)
        tab_f = table.astype(jnp.float32)
        inv_tab = lax.rsqrt(jnp.mean(tab_f * tab_f, axis=-1, keepdims=True) + NORM_EPS)
        n_tab = (tab_f * inv_tab * gain_f).astype(jnp.bfloat16)
        ids_flat = token_ids.reshape(tokens_all)
        normed = jnp.take(n_tab, ids_flat, axis=0)
        u_all = jnp.dot(normed, w_loc, preferred_element_type=jnp.float32).astype(jnp.bfloat16)
        grad_w = lax.dot_general(normed, du_flat, (((0,), (0,)), ((), ())), preferred_element_type=jnp.float32)

        own_ids = lax.dynamic_slice_in_dim(token_ids, dev_idx * seq_loc, seq_loc, axis=1)
        x_own = jnp.take(table, own_ids, axis=0)
        x_f = x_own.astype(jnp.float32)
        inv_own = lax.rsqrt(jnp.mean(x_f * x_f, axis=-1, keepdims=True) + NORM_EPS)
        hat_own = x_f * inv_own
        gain_dn = gain_f * d_norm
        centre = jnp.mean(hat_own * gain_dn, axis=-1, keepdims=True)
        d_x = (dres_loc.astype(jnp.float32) + inv_own * (gain_dn - hat_own * centre)).astype(jnp.bfloat16)
        grad_gain = lax.psum(jnp.sum(d_norm * hat_own, axis=(0, 1)), 'tp')
        dx_all = lax.all_gather(d_x, 'tp', axis=1, tiled=True).reshape(tokens_all, model_dim)
        pick = (ids_flat[None, :] == dev_idx * rows_loc + lax.broadcasted_iota(jnp.int32, (rows_loc, tokens_all), 0)).astype(jnp.bfloat16)
        grad_table = jnp.dot(pick, dx_all, preferred_element_type=jnp.float32)
        return u_all.reshape(num_micro, seq_len, cols_loc), x_own, grad_table, grad_w, grad_gain

    return jax.shard_map(local_step, mesh=mesh,
                         in_specs=(P('dp', None), P('tp', None), P(None), P(None, 'tp'), P('dp', None, 'tp'), P('dp', 'tp', None)),
                         out_specs=(P('dp', None, 'tp'), P('dp', 'tp', None), P(('dp', 'tp'), None), P(None, ('dp', 'tp')), P('dp')),
                         check_vma=False)
```

time: 331 us -> 213 us (0.64)
  matrix products: 141 us -> 87.8 us
  waiting for transfers between devices: 83.5 us -> 50.4 us
  other arithmetic: 43.9 us -> 13.9 us
  starting transfers between devices: 9.9 us -> 5.67 us
    psum x2 -> x0, waiting for transfers between devices: 83.4 us -> none  [micro_step(): tokens = lax.psum(partial_x, 'tp')]
    dot_general x6 -> x4, matrix products: 141 us -> 87.8 us  [the longest x1 32.8 us: local_step(): lax.dot_general(normed, du_flat, (((0,), (0,)), ((), ())), preferred_elem...]
    all_to_all x2 -> x1, waiting for transfers between devices: 0.01 us -> 49.6 us  [local_step(): dn_recv = lax.all_to_all(dn_part, 'tp', 0, 0, tiled=True)]
    scatter-add x2 -> x0, other arithmetic: 15.3 us -> none  [micro_step(): jax.ops.segment_sum(contrib, safe_ids, num_segments=rows_loc)]
    mul x2 -> x0, other arithmetic: 8.24 us -> none  [micro_step(): n_hat = tok_f * inv_rms]
    gather x2, local copies, waits for them, and re-layouts: 9.99 us -> 15.4 us  [the longest x1 11.3 us: local_step(): normed = jnp.take(n_tab, ids_flat, axis=0)]
    select_n x4 -> x1, other arithmetic: 4.79 us -> 0.01 us  [local_step(): normed = jnp.take(n_tab, ids_flat, axis=0)]
    all_to_all x2 -> x1, starting transfers between devices: 9.81 us -> 5.59 us  [local_step(): dn_recv = lax.all_to_all(dn_part, 'tp', 0, 0, tiled=True)]
  transfers between devices with their start and end apart: 6 -> 3, of which waited for: 2 -> 1; matrix products, arithmetic and copies ran while one was open for 47% -> 50% of each run, Pallas kernels for 0% -> 0%
where the time goes in v1:
time: 213 us
  matrix products  87.8 us (41%)
  waiting for transfers between devices  50.4 us (24%)
  blocking collectives  23.1 us (11%)
  local copies, waits for them, and re-layouts  17.8 us (8%)
  between operations  14.2 us (7%)
  other arithmetic  13.9 us (7%)
  starting transfers between devices  5.67 us (3%)
    all_to_all x1, waiting for transfers between devices, local_step(): dn_recv = lax.all_to_all(dn_part, 'tp', 0, 0, tiled=True)  49.6 us
    dot_general x1, matrix products, local_step(): lax.dot_general(normed, du_flat, (((0,), (0,)), ((), ())), preferred_elem...  32.8 us
    dot_general x1, matrix products, local_step(): jnp.dot(normed, w_loc, preferred_element_type=jnp.float32)  27 us
    dot_general x1, matrix products, local_step(): lax.dot_general(du_flat, w_loc, (((1,), (1,)), ((), ())), preferred_eleme...  24 us
    psum x1, blocking collectives, local_step(): grad_gain = lax.psum(jnp.sum(d_norm * hat_own, axis=(0, 1)), 'tp')  23.1 us
    gather x1, local copies, waits for them, and re-layouts, local_step(): normed = jnp.take(n_tab, ids_flat, axis=0)  11.3 us
    convert_element_type x1, other arithmetic, local_step(): n_tab = (tab_f * inv_tab * gain_f).astype(jnp.bfloat16)  5.84 us
    all_to_all x1, starting transfers between devices, local_step(): dn_recv = lax.all_to_all(dn_part, 'tp', 0, 0, tiled=True)  5.59 us
  transfers between devices with their start and end apart: 3, of which 1 were waited for; matrix products, arithmetic and copies ran while one was open for 50% of the time, Pallas kernels for 0%

profile of v1, /device:TPU:0, one launch (start us, length us, event | category | flops | bytes accessed | tf_op | source)
XLA Modules:
  0.0 212.8 jit_solution(17934839860983155228)
XLA Ops:
  7.2 0.0 all-gather.3.cloned.1.call-start
  7.2 0.7 all-gather.3.cloned.1.call-update
  7.9 24.0 %convolution_convert_fusion.1 = bf16[512,4096]{1,0:T(8,128)(2,1)S(1)} fusion(bf16[512,4352]{1,0:T(8,128)(2,1)} %bitcast.30, bf16[4096,4352]{1,0:T(8,128)(2,1)} %param.9), kind=kOutput, calls=%fused_computation.9 | convolution fusion | flops 18255708160 | bytes 44302336 | tf_op jit(solution)/shard_map/dot_general | solution.py:22
  31.9 2.3 %copy.15 = bf16[2,8,32,4096]{3,2,0,1:T(8,128)(2,1)} copy(bf16[2,8,32,4096]{3,2,1,0:T(8,128)(2,1)S(1)} %bitcast.22) | data formatting | bytes 8388608 | tf_op jit(solution)/shard_map/reshape | solution.py:23
  34.2 0.0 copy-start.2
  34.2 0.0 copy-start.3
  34.2 5.6 %all-to-all-start = ((bf16[8,2,32,4096]{3,2,1,0:T(8,128)(2,1)}), bf16[8,2,32,4096]{3,2,1,0:T(8,128)(2,1)}, u32[]{:S(2)}, u32[]{:S(2)}) async-start(bf16[8,2,32,4096]{3,2,1,0:T(8,128)(2,1)} %bitcast.20), calls=%async_computation | async-start | bytes 8388608 | tf_op jit(solution)/shard_map/all_to_all | solution.py:24
  39.8 0.0 all-gather.5.cloned.1.call-start
  39.9 0.0 copy-done.2
  39.9 0.1 compare_and_fusion
  39.9 0.1 reshape.105
  40.0 0.0 copy-done.3
  40.1 49.6 %all-to-all-done = bf16[8,2,32,4096]{3,2,1,0:T(8,128)(2,1)} async-done(((bf16[8,2,32,4096]{3,2,1,0:T(8,128)(2,1)}), bf16[8,2,32,4096]{3,2,1,0:T(8,128)(2,1)}, u32[]{:S(2)}, u32[]{:S(2)}) %all-to-all-start) | async-done | bytes 4194336 | tf_op jit(solution)/shard_map/all_to_all | solution.py:24
  89.8 3.0 %convert_reduce_fusion = f32[2,32,4096]{2,1,0:T(8,128)S(1)} fusion(bf16[8,2,32,4096]{3,2,1,0:T(8,128)(2,1)} %all-to-all-done), kind=kLoop, calls=%fused_computation.7 | loop fusion | flops 3932160 | bytes 5242880 | tf_op jit(solution)/shard_map/reduce_sum | solution.py:25
  92.8 0.0 all-gather.3.cloned.1.call-done
  92.8 3.1 %fusion = f32[512]{0:T(512)S(1)} fusion(bf16[512,4096]{1,0:T(8,128)(2,1)} %all-gather.3.cloned.1.call-done), kind=kLoop, calls=%fused_computation.4 | loop fusion | flops 6290944 | bytes 4196352 | tf_op jit(solution)/shard_map/reduce_sum | solution.py:29
  95.9 0.0 copy-start.1
  95.9 4.2 %gather_fusion.1 = bf16[64,4096]{1,0:T(8,128)(2,1)S(1)} fusion(bf16[512,4096]{1,0:T(8,128)(2,1)} %all-gather.3.cloned.1.call-done, s32[1024]{0:T(1024)S(1)} %pad_clamp_fusion), kind=kCustom, calls=%fused_computation.1 | custom fusion | bytes 1048832 | tf_op jit(solution)/shard_map/jit(_take)/gather | solution.py:37
  100.1 0.3 fusion.13
  100.4 0.0 copy-start
  100.4 0.4 fusion.12
  100.8 23.1 %psum.7 = f32[4096]{0:T(1024)} all-reduce(f32[4096]{0:T(1024)S(1)} %get-tuple-element.5), channel_id=1, replica_groups=mesh['dp'=2,'tp'=8] {'tp'}, use_global_device_ids=true, to_apply=%region_5.6 | all-reduce | flops 4096 | bytes 32768 | tf_op jit(solution)/shard_map/psum | solution.py:44
  123.9 0.0 copy-done.1
  123.9 1.1 fusion.11
  125.0 0.0 all-gather.5.cloned.1.call-update
  125.0 5.8 %fusion.2 = bf16[512,4096]{1,0:T(8,128)(2,1)} fusion(bf16[512,4096]{1,0:T(8,128)(2,1)} %all-gather.3.cloned.1.call-done, f32[4096]{0:T(1024)S(1)} %convert_element_type.29, f32[512]{0:T(512)S(1)} %add_rsqrt_fusion), kind=kLoop, calls=%fused_computation.6 | loop fusion | flops 8388608 | bytes 8407040 | tf_op jit(solution)/shard_map/convert_element_type | solution.py:30
  130.9 0.0 copy-done
  130.9 11.3 %gather_fusion = bf16[512,4096]{1,0:T(8,128)(2,1)} fusion(bf16[512,4096]{1,0:T(8,128)(2,1)} %fusion.2, s32[1024]{0:T(1024)S(1)} %pad_clamp_fusion.1), kind=kCustom, calls=%fused_computation | custom fusion | bytes 8390656 | tf_op jit(solution)/shard_map/jit(_take)/gather | solution.py:32
  142.2 32.8 %fusion.3 = f32[4096,4352]{1,0:T(8,128)} fusion(bf16[512,4352]{1,0:T(8,128)(2,1)} %bitcast.31, bf16[512,4096]{1,0:T(8,128)(2,1)} %gather_fusion, pred[512]{0:T(512)(128)(4,1)S(1)} %compare_and_fusion.1), kind=kOutput, calls=%fused_computation.12 | convolution fusion | flops 18255708160 | bytes 79954432 | tf_op jit(solution)/shard_map/dot_general | solution.py:34
  175.0 27.0 %convolution_convert_fusion = bf16[512,4352]{1,0:T(8,128)(2,1)} fusion(bf16[4096,4352]{1,0:T(8,128)(2,1)} %param.9, bf16[512,4096]{1,0:T(8,128)(2,1)} %gather_fusion, pred[512]{0:T(512)(128)(4,1)S(1)} %compare_and_fusion.1), kind=kOutput, calls=%fused_computation.8 | convolution fusion | flops 18257936384 | bytes 44302848 | tf_op jit(solution)/shard_map/dot_general | solution.py:33
  201.9 0.0 all-gather.5.cloned.1.call-done
  202.0 4.0 %fusion.14 = f32[64,4096]{1,0:T(8,128)} fusion(bf16[512,4096]{1,0:T(8,128)(2,1)} %bitcast.21, s32[512]{0:T(512)S(1)} %bitcast.25, s32[64]{0:T(128)S(1)} %iota_add_fusion), kind=kOutput, calls=%fused_computation.26 | convolution fusion | flops 268468224 | bytes 5245184 | tf_op jit(solution)/shard_map/dot_general | solution.py:47
  (11 shorter events, 0.1 us)
Async XLA Ops:
  7.2 85.6 %all-gather.3.cloned.1.call-start = ((), (), s32[]{:S(2)}) async-start(), calls=%async_computation.1 | async-start | bytes 4718592 | tf_op jit(solution)/shard_map/all_gather | solution.py:27
  34.2 5.6 %copy-start.2 = (s32[2,256]{1,0:T(2,128)S(1)}, s32[2,256]{1,0:T(2,128)}, u32[]{:S(2)}) copy-start(s32[2,256]{1,0:T(2,128)} %param.6) | copy-start | bytes 6148
  34.2 5.8 %copy-start.3 = (bf16[4096]{0:T(1024)(128)(2,1)S(1)}, bf16[4096]{0:T(1024)(128)(2,1)}, u32[]{:S(2)}) copy-start(bf16[4096]{0:T(1024)(128)(2,1)} %param.8) | copy-start | bytes 24580
  34.2 55.5 %all-to-all-start = ((bf16[8,2,32,4096]{3,2,1,0:T(8,128)(2,1)}), bf16[8,2,32,4096]{3,2,1,0:T(8,128)(2,1)}, u32[]{:S(2)}, u32[]{:S(2)}) async-start(bf16[8,2,32,4096]{3,2,1,0:T(8,128)(2,1)} %bitcast.20), calls=%async_computation | async-start | bytes 8388608 | tf_op jit(solution)/shard_map/all_to_all | solution.py:24
  39.8 162.1 %all-gather.5.cloned.1.call-start = ((), (), s32[]{:S(2)}) async-start(), calls=%async_computation.2 | async-start | bytes 4718592 | tf_op jit(solution)/shard_map/all_gather | solution.py:45
  95.9 28.0 %copy-start.1 = (bf16[2,32,4096]{2,1,0:T(8,128)(2,1)S(1)}, bf16[2,32,4096]{2,1,0:T(8,128)(2,1)}, u32[]{:S(2)}) copy-start(bf16[2,32,4096]{2,1,0:T(8,128)(2,1)} %param.11) | copy-start | bytes 1572868
  100.4 30.5 %copy-start = (bf16[2,32,4096]{2,1,0:T(8,128)(2,1)}, bf16[2,32,4096]{2,1,0:T(8,128)(2,1)S(1)}, u32[]{:S(2)}) copy-start(bf16[2,32,4096]{2,1,0:T(8,128)(2,1)S(1)} %get-tuple-element.8) | copy-start | bytes 1572868
Sparse Core Ops, SparseCore 0:
  9.8 36.4 all-gather.2
  125.2 31.9 all-gather.4

commit v2 on v1

v2 whole, which is shorter than its diff:
```python
import functools

import jax
import jax.numpy as jnp
from jax import lax
from jax.experimental import pallas as pl
from jax.experimental.pallas import tpu as pltpu
from jax.sharding import PartitionSpec as P

NORM_EPS = 1e-6
MESH = pl.DeviceIdType.MESH
F32 = jnp.float32
BF16 = jnp.bfloat16
FB = 512
NB = 8
UC = 256
TB = 128


def _flip(r, bits):
    for bit in (1, 2, 4):
        if bits & bit:
            r = r + bit - 2 * bit * (lax.rem(lax.div(r, bit), 2))
    return r


def _rcopy(src, dst, ssem, rsem, dev):
    return pltpu.make_async_remote_copy(src_ref=src, dst_ref=dst, send_sem=ssem, recv_sem=rsem,
                                        device_id={"tp": dev}, device_id_type=MESH)


class _Gather:
    def __init__(self, r, buf, ssem, rsem):
        self.r, self.buf, self.ssem, self.rsem = r, buf, ssem, rsem
        self.sent = 0

    def chunk(self, owner, h):
        return self.buf.at[owner, pl.ds(32 * h, 32)]

    def send(self, rel_owner, h, to, idx, src=None):
        owner = _flip(self.r, rel_owner)
        src = self.chunk(owner, h) if src is None else src
        return _rcopy(src, self.chunk(owner, h), self.ssem.at[idx], self.rsem.at[2 * (rel_owner ^ to) + h],
                      _flip(self.r, to))

    def wait_in(self, rel_owner, h):
        owner = _flip(self.r, rel_owner)
        _rcopy(self.chunk(owner, h), self.chunk(owner, h), self.ssem.at[0], self.rsem.at[2 * rel_owner + h],
               _flip(self.r, 1)).wait_recv()

    def own(self, src=None):
        def s(h):
            return None if src is None else src.at[pl.ds(32 * h, 32)]
        self.send(0, 0, 2, 0, s(0)).start()
        self.send(0, 1, 4, 1, s(1)).start()
        self.send(0, 1, 2, 2, s(1)).start()
        self.send(0, 0, 4, 3, s(0)).start()
        self.send(0, 0, 1, 4, s(0)).start()
        self.send(0, 1, 1, 5, s(1)).start()

    def fwd1(self):
        self.wait_in(2, 0)
        self.send(2, 0, 4, 6).start()
        self.send(2, 0, 1, 7).start()
        self.wait_in(4, 1)
        self.send(4, 1, 2, 8).start()
        self.send(4, 1, 1, 9).start()

    def fwd2(self):
        self.wait_in(2, 1)
        self.send(2, 1, 1, 10).start()
        self.wait_in(4, 0)
        self.send(4, 0, 1, 11).start()

    def fwd3(self):
        self.wait_in(6, 0)
        self.send(6, 0, 1, 12).start()
        self.wait_in(6, 1)
        self.send(6, 1, 1, 13).start()

    def finish(self):
        for rel in (1, 3, 5, 7):
            for h in (0, 1):
                self.wait_in(rel, h)
        for idx in range(14):
            self.send(0, 0, 1, idx).wait_send()


def _k1(idcol, idrow, gain, tab, w, du, dres, u_out, x_out, n_out, de_out, dg_out,
        du_v, w_v, etab, dn_v, rx1, tx2, rx2, own, wc_v, u_v, n_v, nh_v, x_v, dres_v, dx_all, dgs,
        lsem, wsem, wcsem, usem, e_s, e_r, s1, r1, s2, r2, a_s, a_r, g_s, g_r):
    r = lax.axis_index("tp")
    core = lax.rem(r, 2)
    xs = lax.rem(lax.div(r, 2), 2)
    ys = lax.div(r, 4)
    cols = w.shape[1]
    n_u = cols // UC

    du_cp = [pltpu.make_async_copy(du.at[m], du_v.at[:, m], lsem.at[m]) for m in range(2)]
    for c in du_cp:
        c.start()

    def w_cp(j, slot):
        return pltpu.make_async_copy(w.at[pl.ds(pl.multiple_of(j * FB, FB), FB)], w_v.at[slot], wsem.at[slot])

    def wc_cp(i, slot):
        return pltpu.make_async_copy(w.at[:, pl.ds(pl.multiple_of(i * UC, UC), UC)], wc_v.at[slot], wcsem.at[slot])

    def u_cp(i, slot):
        return pltpu.make_async_copy(u_v.at[slot], u_out.at[:, pl.ds(pl.multiple_of(i * UC, UC), UC)], usem.at[slot])

    w_cp(0, 0).start()
    tab_cp = pltpu.make_async_copy(tab, etab.at[r], lsem.at[2])
    tab_cp.start()
    dres_cp = pltpu.make_async_copy(dres, dres_v, lsem.at[3])
    dres_cp.start()

    barrier = pltpu.get_barrier_semaphore()
    for rel in range(1, 8):
        pl.semaphore_signal(barrier, inc=1, device_id={"tp": _flip(r, rel)}, device_id_type=MESH)
    pl.semaphore_wait(barrier, 7)

    eg = _Gather(r, etab, e_s, e_r)
    eg.own(tab)
    for c in du_cp:
        c.wait()

    def rs1(j, even):
        if even:
            sib = dn_v.at[j, :, xs, 1 - core]
            far = [dn_v.at[j, :, 1 - xs, c] for c in range(2)]
            dev = [(ys * 2 + 1 - xs) * 2 + c for c in range(2)]
        else:
            sib = dn_v.at[j, ys, :, 1 - core]
            far = [dn_v.at[j, 1 - ys, :, c] for c in range(2)]
            dev = [((1 - ys) * 2 + xs) * 2 + c for c in range(2)]
        out = [_rcopy(far[c], rx1.at[j, 1 + core], s1.at[j, 1 + c], r1.at[j, 1 + core], dev[c]) for c in range(2)]
        out.append(_rcopy(sib, rx1.at[j, 0], s1.at[j, 0], r1.at[j, 0], _flip(r, 1)))
        return out

    def rs1_start(j):
        @pl.when(lax.rem(j, 2) == 0)
        def _():
            for c in rs1(j, True):
                c.start()

        @pl.when(lax.rem(j, 2) == 1)
        def _():
            for c in rs1(j, False):
                c.start()

    def other(j):
        odd = lax.rem(j, 2)
        oy = ys + (1 - 2 * ys) * (1 - odd)
        ox = xs + (1 - 2 * xs) * odd
        q = ys * (1 - odd) + xs * odd
        return oy, ox, q

    def combine(j):
        oy, ox, q = other(j)
        for s in range(3):
            _rcopy(rx1.at[j, s], rx1.at[j, s], s1.at[j, 0], r1.at[j, s], _flip(r, 1)).wait_recv()

        def total(part, qi):
            t = part.astype(F32)
            for s in range(3):
                t = t + rx1[j, s, qi].astype(F32)
            return t

        tx2[j] = total(dn_v[j, oy, ox, core], 1 - q)
        own[j] = total(dn_v[j, ys, xs, core], q)

    def rs2(j):
        oy, ox, _ = other(j)
        return _rcopy(tx2.at[j], rx2.at[j], s2.at[j], r2.at[j], (oy * 2 + ox) * 2 + core)

    def dn_step(j, carry):
        slot = lax.rem(j, 2)
        w_cp(j, slot).wait()

        @pl.when(j + 1 < NB)
        def _():
            w_cp(j + 1, 1 - slot).start()

        part = lax.dot_general(du_v[...].reshape(512, cols), w_v[slot], (((1,), (1,)), ((), ())),
                               preferred_element_type=F32)
        dn_v[j] = part.astype(BF16).reshape(2, 2, 2, 64, FB)

        @pl.when(j == 3)
        def _():
            eg.fwd1()
            for jj in range(3):
                rs1_start(jj)

        @pl.when(j > 3)
        def _():
            rs1_start(j - 1)

        @pl.when(j == 6)
        def _():
            eg.fwd2()
            wc_cp(0, 0).start()

        return carry

    lax.fori_loop(0, NB, dn_step, 0)
    tab_cp.wait()
    eg.fwd3()
    rs1_start(NB - 1)
    eg.finish()

    gf = gain[...].astype(F32)
    lanes = lax.broadcasted_iota(jnp.int32, (TB, 512), 1)

    def lookup(ids, rows):
        pick = (ids == lanes[:rows]).astype(BF16)
        return jnp.dot(pick, etab[...].reshape(512, 4096), preferred_element_type=F32)

    def n_step(b, carry):
        rows = pl.ds(pl.multiple_of(b * TB, TB), TB)
        xg = lookup(idcol[rows, :], TB)
        inv = lax.rsqrt(jnp.mean(xg * xg, axis=-1, keepdims=True) + NORM_EPS)
        n_v[rows, :] = (xg * inv * gf).astype(BF16)
        return carry

    lax.fori_loop(0, 512 // TB, n_step, 0)
    n_cp = pltpu.make_async_copy(n_v, n_out, lsem.at[0])
    n_cp.start()

    start = pl.multiple_of(r * 32, 32)
    own_ids = jnp.concatenate([idcol[pl.ds(start, 32), :], idcol[pl.ds(start + 256, 32), :]], axis=0)
    xo = lookup(own_ids, 64)
    inv_own = lax.rsqrt(jnp.mean(xo * xo, axis=-1, keepdims=True) + NORM_EPS)
    x_v[...] = xo.astype(BF16).reshape(2, 32, 4096)
    nh_v[...] = xo * inv_own
    x_cp = pltpu.make_async_copy(x_v, x_out, lsem.at[1])
    x_cp.start()

    def u_step(i, carry):
        slot = lax.rem(i, 2)
        wc_cp(i, slot).wait()

        @pl.when(i + 1 < n_u)
        def _():
            wc_cp(i + 1, 1 - slot).start()

        @pl.when(i >= 2)
        def _():
            u_cp(i - 2, slot).wait()

        u_v[slot] = jnp.dot(n_v[...], wc_v[slot], preferred_element_type=F32).astype(BF16)
        u_cp(i, slot).start()

        pair = lax.div(i, 5) - 1

        @pl.when((lax.rem(i, 5) == 0) & (i > 0))
        def _():
            combine(2 * pair)
            combine(2 * pair + 1)

        @pl.when((lax.rem(i, 5) == 1) & (i > 1))
        def _():
            rs2(2 * pair).start()
            rs2(2 * pair + 1).start()

        return carry

    lax.fori_loop(0, n_u, u_step, 0)
    combine(6)
    combine(7)
    dres_cp.wait()
    u_cp(n_u - 2, lax.rem(n_u - 2, 2)).wait()
    u_cp(n_u - 1, lax.rem(n_u - 1, 2)).wait()
    rs2(6).start()
    rs2(7).start()

    centre = jnp.zeros((64, 1), F32)
    for j in range(NB):
        sl = slice(j * FB, (j + 1) * FB)
        rs2(j).wait_recv()
        dn = own[j] + rx2[j]
        own[j] = dn
        nh = nh_v[:, sl]
        centre = centre + jnp.sum(nh * (gf[:, sl] * dn), axis=-1, keepdims=True)
        dgs[r, :, sl] = jnp.sum(dn * nh, axis=0, keepdims=True)
    centre = centre * (1.0 / 4096)
    for j in range(NB):
        sl = slice(j * FB, (j + 1) * FB)
        dr = dres_v[:, :, sl].reshape(64, FB).astype(F32)
        dx = dr + inv_own * (gf[:, sl] * own[j] - nh_v[:, sl] * centre)
        dx_all[r, :, sl] = dx.astype(BF16)

    def dg_cp(rel):
        return _rcopy(dgs.at[r], dgs.at[r], g_s.at[rel], g_r.at[r], _flip(r, rel))

    for rel in range(1, 8):
        dg_cp(rel).start()
    ag = _Gather(r, dx_all, a_s, a_r)
    ag.own()
    ag.fwd1()
    ag.fwd2()
    ag.fwd3()
    for rel in range(1, 8):
        src = _flip(r, rel)
        _rcopy(dgs.at[src], dgs.at[src], g_s.at[rel], g_r.at[src], src).wait_recv()
    tot = dgs[0]
    for k in range(1, 8):
        tot = tot + dgs[k]
    dg_out[...] = tot
    pick = (idrow[...] == r * 64 + lax.broadcasted_iota(jnp.int32, (64, 512), 0)).astype(BF16)
    ag.finish()
    de_out[...] = jnp.dot(pick, dx_all[...].reshape(512, 4096), preferred_element_type=F32)

    for rel in range(1, 8):
        dg_cp(rel).wait_send()
    for j in range(NB):
        for c in rs1(j, j % 2 == 0):
            c.wait_send()
        rs2(j).wait_send()
    n_cp.wait()
    x_cp.wait()


def solution(mesh):
    group_size = mesh.shape['tp']

    def local_step(token_ids, table_loc, gain_vec, w_loc, du_loc, dres_loc):
        num_micro, seq_len = token_ids.shape
        rows_loc, model_dim = table_loc.shape
        seq_loc = seq_len // group_size
        cols_loc = w_loc.shape[1]
        tokens = num_micro * seq_len
        du_flat = du_loc.reshape(tokens, cols_loc)
        idcol = token_ids.reshape(tokens, 1)
        idrow = token_ids.reshape(num_micro, group_size, seq_loc).transpose(1, 0, 2).reshape(1, tokens)
        vm, hb = pl.BlockSpec(memory_space=pltpu.VMEM), pl.BlockSpec(memory_space=pl.ANY)
        sd = jax.ShapeDtypeStruct
        dma = pltpu.SemaphoreType.DMA
        u_all, x_own, normed, grad_table, grad_gain = pl.pallas_call(
            _k1,
            out_shape=(sd((tokens, cols_loc), BF16), sd((num_micro, seq_loc, model_dim), BF16),
                       sd((tokens, model_dim), BF16), sd((rows_loc, model_dim), F32), sd((1, model_dim), F32)),
            in_specs=[vm, vm, vm, hb, hb, hb, hb],
            out_specs=(hb, hb, hb, vm, vm),
            scratch_shapes=[
                pltpu.VMEM((8, 2, 32, cols_loc), BF16),
                pltpu.VMEM((2, FB, cols_loc), BF16),
                pltpu.VMEM((8, 64, model_dim), BF16),
                pltpu.VMEM((NB, 2, 2, 2, 64, FB), BF16),
                pltpu.VMEM((NB, 3, 2, 64, FB), BF16),
                pltpu.VMEM((NB, 64, FB), F32),
                pltpu.VMEM((NB, 64, FB), F32),
                pltpu.VMEM((NB, 64, FB), F32),
                pltpu.VMEM((2, model_dim, UC), BF16),
                pltpu.VMEM((2, tokens, UC), BF16),
                pltpu.VMEM((tokens, model_dim), BF16),
                pltpu.VMEM((64, model_dim), F32),
                pltpu.VMEM((2, 32, model_dim), BF16),
                pltpu.VMEM((2, 32, model_dim), BF16),
                pltpu.VMEM((8, 64, model_dim), BF16),
                pltpu.VMEM((8, 1, model_dim), F32),
                dma((4,)), dma((2,)), dma((2,)), dma((2,)),
                dma((14,)), dma((16,)),
                dma((NB, 3)), dma((NB, 3)), dma((NB,)), dma((NB,)),
                dma((14,)), dma((16,)),
                dma((8,)), dma((8,)),
            ],
            compiler_params=pltpu.CompilerParams(collective_id=0, has_side_effects=True,
                                                 vmem_limit_bytes=60 * 2 ** 20),
            name="k1",
        )(idcol, idrow, gain_vec.reshape(1, model_dim), table_loc, w_loc,
          du_loc.reshape(num_micro, group_size, seq_loc, cols_loc), dres_loc)
        grad_w = lax.dot_general(normed, du_flat, (((0,), (0,)), ((), ())), preferred_element_type=F32)
        return u_all.reshape(num_micro, seq_len, cols_loc), x_own, grad_table, grad_w, grad_gain.reshape(model_dim)

    return jax.shard_map(local_step, mesh=mesh,
                         in_specs=(P('dp', None), P('tp', None), P(None), P(None, 'tp'), P('dp', None, 'tp'), P('dp', 'tp', None)),
                         out_specs=(P('dp', None, 'tp'), P('dp', 'tp', None), P(('dp', 'tp'), None), P(None, ('dp', 'tp')), P('dp')),
                         check_vma=False)
```

time: 213 us -> 141 us (0.66)
  Pallas kernels: 0 us -> 95 us
  matrix products: 87.8 us -> 32.9 us
  waiting for transfers between devices: 50.4 us -> 0 us
  blocking collectives: 23.1 us -> 0 us
  other arithmetic: 13.9 us -> 0 us
  between operations: 14.2 us -> 0.65 us
  local copies, waits for them, and re-layouts: 17.8 us -> 11.4 us
  starting transfers between devices: 5.67 us -> 0 us
    pallas_call x0 -> x1, Pallas kernels: none -> 95 us  [local_step(): pl.pallas_call(_k1, out_shape=(sd((tokens, cols_loc), BF16), sd((num_micr...]
    dot_general x3 -> x0, matrix products: 55 us -> none  [the longest x1 27 us: local_step(): jnp.dot(normed, w_loc, preferred_element_type=jnp.float32)]
    all_to_all x1 -> x0, waiting for transfers between devices: 49.6 us -> none  [local_step(): dn_recv = lax.all_to_all(dn_part, 'tp', 0, 0, tiled=True)]
    psum x1 -> x0, blocking collectives: 23.1 us -> none  [local_step(): grad_gain = lax.psum(jnp.sum(d_norm * hat_own, axis=(0, 1)), 'tp')]
    gather x2 -> x0, local copies, waits for them, and re-layouts: 15.4 us -> none  [the longest x1 11.3 us: local_step(): normed = jnp.take(n_tab, ids_flat, axis=0)]
    unnamed x10 -> x12, local copies, waits for them, and re-layouts: 0.02 us -> 8.69 us
    convert_element_type x3 -> x0, other arithmetic: 6.98 us -> none  [the longest x1 5.84 us: local_step(): n_tab = (tab_f * inv_tab * gain_f).astype(jnp.bfloat16)]
    reduce_sum x4 -> x0, other arithmetic: 6.8 us -> none  [the longest x1 3.08 us: local_step(): jnp.mean(tab_f * tab_f, axis=-1, keepdims=True) + NORM_EPS]
  transfers between devices with their start and end apart: 3 -> 0, of which waited for: 1 -> 0; matrix products, arithmetic and copies ran while one was open for 50% -> 0% of each run, Pallas kernels for 0% -> 0%
where the time goes in v2:
time: 141 us; the launch traced here: 140 us
  Pallas kernels  95 us (67%)
  matrix products  32.9 us (23%)
  local copies, waits for them, and re-layouts  11.4 us (8%)
    pallas_call x1, Pallas kernels, local_step(): pl.pallas_call(_k1, out_shape=(sd((tokens, cols_loc), BF16), sd((num_micr...  95 us
    dot_general x1, matrix products, local_step(): lax.dot_general(normed, du_flat, (((0,), (0,)), ((), ())), preferred_elem...  32.9 us
    unnamed x12, local copies, waits for them, and re-layouts  8.69 us

profile of v2, /device:TPU:0, one launch (start us, length us, event | category | flops | bytes accessed | tf_op | source)
XLA Modules:
  0.0 140.0 jit_solution(6637728983875822487)
XLA Ops:
  0.6 0.7 copy.14
  1.3 0.8 reshape.35
  2.1 0.7 reshape.36.idrow
  2.7 1.3 reshape.37.gain
  4.1 0.9 copy.15
  4.9 95.0 %k1.1 = (bf16[512,4352]{1,0:T(8,128)(2,1)}, bf16[2,32,4096]{2,1,0:T(8,128)(2,1)}, bf16[512,4096]{1,0:T(8,128)(2,1)}, f32[64,4096]{1,0:T(8,128)}, f32[1,4096]{1,0:T(1,128)}) custom-call(s32[512,1]{1,0:T(8,128)} %bitcast.16, s32[1,512]{1,0:T(1,128)} %reshape.36.idrow, bf16[1,4096]{1,0:T(2,128)(2,1)} %reshape.37.gain, bf16[64,4096]{1,0:T(8,128)(2,1)} %tab.1, ...), custom_call_target="tpu_custom_call" | custom-call | tf_op jit(solution)/shard_map/k1/pallas_call | solution.py:339
  99.9 32.9 %fusion = f32[4096,4352]{1,0:T(8,128)} fusion(bf16[512,4096]{1,0:T(8,128)(2,1)} %get-tuple-element.13, bf16[512,4352]{1,0:T(8,128)(2,1)} %bitcast.14), kind=kOutput, calls=%fused_computation.1 | convolution fusion | flops 18253611008 | bytes 79953920 | tf_op jit(solution)/shard_map/dot_general | solution.py:373
  132.8 0.0 copy-start.1
  132.8 0.0 copy-start
  132.8 0.0 copy-start.2
  132.8 4.8 %copy.22 = bf16[2,256,4352]{2,1,0:T(8,128)(2,1)} copy(bf16[2,256,4352]{2,1,0:T(8,128)(2,1)} %bitcast.15) | data formatting | bytes 8912896
  137.6 0.0 copy-done.1
  137.6 0.8 copy.23
  138.4 0.0 copy-done
  138.4 1.0 copy.24
  139.3 0.0 copy-done.2
  139.3 0.6 copy.25
  (1 shorter events, 0.0 us)
Async XLA Ops:
  132.8 4.8 %copy-start.1 = (bf16[2,32,4096]{2,1,0:T(8,128)(2,1)S(1)}, bf16[2,32,4096]{2,1,0:T(8,128)(2,1)}, u32[]{:S(2)}) copy-start(bf16[2,32,4096]{2,1,0:T(8,128)(2,1)} %get-tuple-element.21) | copy-start | bytes 1572868
  132.8 5.6 %copy-start = (f32[64,4096]{1,0:T(8,128)S(1)}, f32[64,4096]{1,0:T(8,128)}, u32[]{:S(2)}) copy-start(f32[64,4096]{1,0:T(8,128)} %get-tuple-element.22) | copy-start | bytes 3145732
  132.8 6.5 %copy-start.2 = (f32[1,4096]{1,0:T(1,128)S(1)}, f32[1,4096]{1,0:T(1,128)}, u32[]{:S(2)}) copy-start(f32[1,4096]{1,0:T(1,128)} %get-tuple-element.14) | copy-start | bytes 49156

commit v3 on v2

--- a/solution.py
+++ b/solution.py
@@ -15,6 +15,8 @@
 NB = 8
 UC = 256
 TB = 128
+WS = 3
+CS = 4
 
 
 def _flip(r, bits):
@@ -30,12 +32,8 @@
 
 
 class _Gather:
-    def __init__(self, r, buf, ssem, rsem):
-        self.r, self.buf, self.ssem, self.rsem = r, buf, ssem, rsem
-        self.sent = 0
-
-    def chunk(self, owner, h):
-        return self.buf.at[owner, pl.ds(32 * h, 32)]
+    def __init__(self, r, chunk, ssem, rsem):
+        self.r, self.chunk, self.ssem, self.rsem = r, chunk, ssem, rsem
 
     def send(self, rel_owner, h, to, idx, src=None):
         owner = _flip(self.r, rel_owner)
@@ -86,7 +84,7 @@
             self.send(0, 0, 1, idx).wait_send()
 
 
-def _k1(idcol, idrow, gain, tab, w, du, dres, u_out, x_out, n_out, de_out, dg_out,
+def _k1(ids, gain, tab, w, du, dres, u_out, x_out, n_out, de_out, dg_out,
         du_v, w_v, etab, dn_v, rx1, tx2, rx2, own, wc_v, u_v, n_v, nh_v, x_v, dres_v, dx_all, dgs,
         lsem, wsem, wcsem, usem, e_s, e_r, s1, r1, s2, r2, a_s, a_r, g_s, g_r):
     r = lax.axis_index("tp")
@@ -109,7 +107,8 @@
     def u_cp(i, slot):
         return pltpu.make_async_copy(u_v.at[slot], u_out.at[:, pl.ds(pl.multiple_of(i * UC, UC), UC)], usem.at[slot])
 
-    w_cp(0, 0).start()
+    for k in range(WS - 1):
+        w_cp(k, k).start()
     tab_cp = pltpu.make_async_copy(tab, etab.at[r], lsem.at[2])
     tab_cp.start()
     dres_cp = pltpu.make_async_copy(dres, dres_v, lsem.at[3])
@@ -120,7 +119,7 @@
         pl.semaphore_signal(barrier, inc=1, device_id={"tp": _flip(r, rel)}, device_id_type=MESH)
     pl.semaphore_wait(barrier, 7)
 
-    eg = _Gather(r, etab, e_s, e_r)
+    eg = _Gather(r, lambda owner, h: etab.at[owner, pl.ds(32 * h, 32)], e_s, e_r)
     eg.own(tab)
     for c in du_cp:
         c.wait()
@@ -175,12 +174,12 @@
         return _rcopy(tx2.at[j], rx2.at[j], s2.at[j], r2.at[j], (oy * 2 + ox) * 2 + core)
 
     def dn_step(j, carry):
-        slot = lax.rem(j, 2)
+        slot = lax.rem(j, WS)
         w_cp(j, slot).wait()
 
-        @pl.when(j + 1 < NB)
-        def _():
-            w_cp(j + 1, 1 - slot).start()
+        @pl.when(j + WS - 1 < NB)
+        def _():
+            w_cp(j + WS - 1, lax.rem(j + WS - 1, WS)).start()
 
         part = lax.dot_general(du_v[...].reshape(512, cols), w_v[slot], (((1,), (1,)), ((), ())),
                                preferred_element_type=F32)
@@ -199,7 +198,8 @@
         @pl.when(j == 6)
         def _():
             eg.fwd2()
-            wc_cp(0, 0).start()
+            for k in range(CS - 1):
+                wc_cp(k, k).start()
 
         return carry
 
@@ -209,27 +209,31 @@
     rs1_start(NB - 1)
     eg.finish()
 
-    gf = gain[...].astype(F32)
-    lanes = lax.broadcasted_iota(jnp.int32, (TB, 512), 1)
-
-    def lookup(ids, rows):
-        pick = (ids == lanes[:rows]).astype(BF16)
-        return jnp.dot(pick, etab[...].reshape(512, 4096), preferred_element_type=F32)
-
-    def n_step(b, carry):
-        rows = pl.ds(pl.multiple_of(b * TB, TB), TB)
-        xg = lookup(idcol[rows, :], TB)
+    gf = gain[...].astype(F32).reshape(1, 4096)
+
+    def one_hot(first, rows, tok):
+        return (tok == first + lax.broadcasted_iota(jnp.int32, (rows, tok.shape[1]), 0)).astype(BF16)
+
+    def lookup(pick_t):
+        return lax.dot_general(pick_t, etab[...].reshape(512, 4096), (((0,), (0,)), ((), ())),
+                               preferred_element_type=F32)
+
+    for b in range(512 // TB):
+        rows = slice(b * TB, (b + 1) * TB)
+        col = b * TB % 256
+        xg = lookup(one_hot(0, 512, ids[b * TB // 256:b * TB // 256 + 1, col:col + TB]))
         inv = lax.rsqrt(jnp.mean(xg * xg, axis=-1, keepdims=True) + NORM_EPS)
         n_v[rows, :] = (xg * inv * gf).astype(BF16)
-        return carry
-
-    lax.fori_loop(0, 512 // TB, n_step, 0)
+
     n_cp = pltpu.make_async_copy(n_v, n_out, lsem.at[0])
     n_cp.start()
 
-    start = pl.multiple_of(r * 32, 32)
-    own_ids = jnp.concatenate([idcol[pl.ds(start, 32), :], idcol[pl.ds(start + 256, 32), :]], axis=0)
-    xo = lookup(own_ids, 64)
+    mine = (lax.broadcasted_iota(jnp.int32, (32, 256), 1) ==
+            r * 32 + lax.broadcasted_iota(jnp.int32, (32, 256), 0)).astype(BF16)
+    pick_own = jnp.concatenate(
+        [lax.dot_general(mine, one_hot(0, 512, ids[m:m + 1, :]), (((1,), (1,)), ((), ())), preferred_element_type=F32)
+         for m in range(2)], axis=0).astype(BF16)
+    xo = jnp.dot(pick_own, etab[...].reshape(512, 4096), preferred_element_type=F32)
     inv_own = lax.rsqrt(jnp.mean(xo * xo, axis=-1, keepdims=True) + NORM_EPS)
     x_v[...] = xo.astype(BF16).reshape(2, 32, 4096)
     nh_v[...] = xo * inv_own
@@ -238,27 +242,28 @@
 
     def u_step(i, carry):
         slot = lax.rem(i, 2)
-        wc_cp(i, slot).wait()
-
-        @pl.when(i + 1 < n_u)
-        def _():
-            wc_cp(i + 1, 1 - slot).start()
+        wslot = lax.rem(i, CS)
+        wc_cp(i, wslot).wait()
+
+        @pl.when(i + CS - 1 < n_u)
+        def _():
+            wc_cp(i + CS - 1, lax.rem(i + CS - 1, CS)).start()
 
         @pl.when(i >= 2)
         def _():
             u_cp(i - 2, slot).wait()
 
-        u_v[slot] = jnp.dot(n_v[...], wc_v[slot], preferred_element_type=F32).astype(BF16)
+        u_v[slot] = jnp.dot(n_v[...], wc_v[wslot], preferred_element_type=F32).astype(BF16)
         u_cp(i, slot).start()
 
-        pair = lax.div(i, 5) - 1
-
-        @pl.when((lax.rem(i, 5) == 0) & (i > 0))
+        pair = lax.div(i, 5)
+
+        @pl.when(lax.rem(i, 5) == 0)
         def _():
             combine(2 * pair)
             combine(2 * pair + 1)
 
-        @pl.when((lax.rem(i, 5) == 1) & (i > 1))
+        @pl.when(lax.rem(i, 5) == 1)
         def _():
             rs2(2 * pair).start()
             rs2(2 * pair + 1).start()
@@ -266,13 +271,9 @@
         return carry
 
     lax.fori_loop(0, n_u, u_step, 0)
-    combine(6)
-    combine(7)
     dres_cp.wait()
     u_cp(n_u - 2, lax.rem(n_u - 2, 2)).wait()
     u_cp(n_u - 1, lax.rem(n_u - 1, 2)).wait()
-    rs2(6).start()
-    rs2(7).start()
 
     centre = jnp.zeros((64, 1), F32)
     for j in range(NB):
@@ -288,14 +289,15 @@
         sl = slice(j * FB, (j + 1) * FB)
         dr = dres_v[:, :, sl].reshape(64, FB).astype(F32)
         dx = dr + inv_own * (gf[:, sl] * own[j] - nh_v[:, sl] * centre)
-        dx_all[r, :, sl] = dx.astype(BF16)
+        for m in range(2):
+            dx_all[m, r, :, sl] = dx[32 * m:32 * m + 32].astype(BF16)
 
     def dg_cp(rel):
         return _rcopy(dgs.at[r], dgs.at[r], g_s.at[rel], g_r.at[r], _flip(r, rel))
 
     for rel in range(1, 8):
         dg_cp(rel).start()
-    ag = _Gather(r, dx_all, a_s, a_r)
+    ag = _Gather(r, lambda owner, h: dx_all.at[h, owner], a_s, a_r)
     ag.own()
     ag.fwd1()
     ag.fwd2()
@@ -307,7 +309,7 @@
     for k in range(1, 8):
         tot = tot + dgs[k]
     dg_out[...] = tot
-    pick = (idrow[...] == r * 64 + lax.broadcasted_iota(jnp.int32, (64, 512), 0)).astype(BF16)
+    pick = jnp.concatenate([one_hot(r * 64, 64, ids[m:m + 1, :]) for m in range(2)], axis=1)
     ag.finish()
     de_out[...] = jnp.dot(pick, dx_all[...].reshape(512, 4096), preferred_element_type=F32)
 
@@ -321,6 +323,14 @@
     x_cp.wait()
 
 
+def _k2(n_ref, du_ref, u_ref, x_ref, de_ref, dg_ref, dw_out, u_out, x_out, de_out, dg_out):
+    dw_out[...] = lax.dot_general(n_ref[...], du_ref[...], (((0,), (0,)), ((), ())), preferred_element_type=F32)
+    u_out[...] = u_ref[...]
+    x_out[...] = x_ref[...]
+    de_out[...] = de_ref[...]
+    dg_out[...] = dg_ref[...]
+
+
 def solution(mesh):
     group_size = mesh.shape['tp']
 
@@ -331,8 +341,6 @@
         cols_loc = w_loc.shape[1]
         tokens = num_micro * seq_len
         du_flat = du_loc.reshape(tokens, cols_loc)
-        idcol = token_ids.reshape(tokens, 1)
-        idrow = token_ids.reshape(num_micro, group_size, seq_loc).transpose(1, 0, 2).reshape(1, tokens)
         vm, hb = pl.BlockSpec(memory_space=pltpu.VMEM), pl.BlockSpec(memory_space=pl.ANY)
         sd = jax.ShapeDtypeStruct
         dma = pltpu.SemaphoreType.DMA
@@ -340,26 +348,26 @@
             _k1,
             out_shape=(sd((tokens, cols_loc), BF16), sd((num_micro, seq_loc, model_dim), BF16),
                        sd((tokens, model_dim), BF16), sd((rows_loc, model_dim), F32), sd((1, model_dim), F32)),
-            in_specs=[vm, vm, vm, hb, hb, hb, hb],
+            in_specs=[vm, vm, hb, hb, hb, hb],
             out_specs=(hb, hb, hb, vm, vm),
             scratch_shapes=[
                 pltpu.VMEM((8, 2, 32, cols_loc), BF16),
-                pltpu.VMEM((2, FB, cols_loc), BF16),
+                pltpu.VMEM((WS, FB, cols_loc), BF16),
                 pltpu.VMEM((8, 64, model_dim), BF16),
                 pltpu.VMEM((NB, 2, 2, 2, 64, FB), BF16),
                 pltpu.VMEM((NB, 3, 2, 64, FB), BF16),
                 pltpu.VMEM((NB, 64, FB), F32),
                 pltpu.VMEM((NB, 64, FB), F32),
                 pltpu.VMEM((NB, 64, FB), F32),
-                pltpu.VMEM((2, model_dim, UC), BF16),
+                pltpu.VMEM((CS, model_dim, UC), BF16),
                 pltpu.VMEM((2, tokens, UC), BF16),
                 pltpu.VMEM((tokens, model_dim), BF16),
                 pltpu.VMEM((64, model_dim), F32),
                 pltpu.VMEM((2, 32, model_dim), BF16),
                 pltpu.VMEM((2, 32, model_dim), BF16),
-                pltpu.VMEM((8, 64, model_dim), BF16),
+                pltpu.VMEM((2, 8, 32, model_dim), BF16),
                 pltpu.VMEM((8, 1, model_dim), F32),
-                dma((4,)), dma((2,)), dma((2,)), dma((2,)),
+                dma((4,)), dma((WS,)), dma((CS,)), dma((2,)),
                 dma((14,)), dma((16,)),
                 dma((NB, 3)), dma((NB, 3)), dma((NB,)), dma((NB,)),
                 dma((14,)), dma((16,)),
@@ -368,9 +376,24 @@
             compiler_params=pltpu.CompilerParams(collective_id=0, has_side_effects=True,
                                                  vmem_limit_bytes=60 * 2 ** 20),
             name="k1",
-        )(idcol, idrow, gain_vec.reshape(1, model_dim), table_loc, w_loc,
+        )(token_ids, gain_vec, table_loc, w_loc,
           du_loc.reshape(num_micro, group_size, seq_loc, cols_loc), dres_loc)
-        grad_w = lax.dot_general(normed, du_flat, (((0,), (0,)), ((), ())), preferred_element_type=F32)
+        steps = 16
+        fb, ub = model_dim // steps, tokens // steps
+        blk = pl.BlockSpec
+        io = [blk((ub, cols_loc), lambda i: (i, 0)), blk((num_micro, seq_loc, fb), lambda i: (0, 0, i)),
+              blk((rows_loc, fb), lambda i: (0, i)), blk((1, fb), lambda i: (0, i))]
+        grad_w, u_all, x_own, grad_table, grad_gain = pl.pallas_call(
+            _k2,
+            grid=(steps,),
+            out_shape=(sd((model_dim, cols_loc), F32), sd((tokens, cols_loc), BF16),
+                       sd((num_micro, seq_loc, model_dim), BF16), sd((rows_loc, model_dim), F32),
+                       sd((1, model_dim), F32)),
+            in_specs=[blk((tokens, fb), lambda i: (0, i)), blk((tokens, cols_loc), lambda i: (0, 0))] + io,
+            out_specs=[blk((fb, cols_loc), lambda i: (i, 0))] + io,
+            compiler_params=pltpu.CompilerParams(dimension_semantics=("arbitrary",), vmem_limit_bytes=60 * 2 ** 20),
+            name="k2",
+        )(normed, du_flat, u_all, x_own, grad_table, grad_gain)
         return u_all.reshape(num_micro, seq_len, cols_loc), x_own, grad_table, grad_w, grad_gain.reshape(model_dim)
 
     return jax.shard_map(local_step, mesh=mesh,

time: 141 us -> 119 us (0.84)
  matrix products: 32.9 us -> 0 us
  Pallas kernels: 95 us -> 118 us
  local copies, waits for them, and re-layouts: 11.4 us -> 0 us
    dot_general x1 -> x0, matrix products: 32.9 us -> none  [local_step(): lax.dot_general(normed, du_flat, (((0,), (0,)), ((), ())), preferred_elem...]
    pallas_call x0 -> x1, Pallas kernels: none -> 32 us  [local_step(): pl.pallas_call(_k2, grid=(steps,), out_shape=(sd((model_dim, cols_loc), F...]
    unnamed x12 -> x0, local copies, waits for them, and re-layouts: 8.69 us -> none
    pallas_call x1, Pallas kernels: 95 us -> 86.3 us  [local_step(): pl.pallas_call(_k1, out_shape=(sd((tokens, cols_loc), BF16), sd((num_micr...]
    reshape x4 -> x0, local copies, waits for them, and re-layouts: 2.74 us -> none  [the longest x3 1.43 us: local_step(): token_ids.reshape(num_micro, group_size, seq_loc).transpose(1, 0, 2)]
where the time goes in v3:
time: 119 us
  Pallas kernels  118 us (99%)
    pallas_call x1, Pallas kernels, local_step(): pl.pallas_call(_k1, out_shape=(sd((tokens, cols_loc), BF16), sd((num_micr...  86.3 us
    pallas_call x1, Pallas kernels, local_step(): pl.pallas_call(_k2, grid=(steps,), out_shape=(sd((model_dim, cols_loc), F...  32 us

profile of v3, /device:TPU:0, one launch (start us, length us, event | category | flops | bytes accessed | tf_op | source)
XLA Modules:
  0.0 119.0 jit_solution(17259771469960257755)
XLA Ops:
  0.6 86.3 %k1.1 = (bf16[512,4352]{1,0:T(8,128)(2,1)}, bf16[2,32,4096]{2,1,0:T(8,128)(2,1)}, bf16[512,4096]{1,0:T(8,128)(2,1)}, f32[64,4096]{1,0:T(8,128)}, f32[1,4096]{1,0:T(1,128)}) custom-call(s32[2,256]{1,0:T(2,128)} %ids.1, bf16[4096]{0:T(1024)(128)(2,1)} %gain.1, bf16[64,4096]{1,0:T(8,128)(2,1)} %tab.1, bf16[4096,4352]{1,0:T(8,128)(2,1)} %w.1, ...), custom_call_target="tpu_custom_call" | custom-call | tf_op jit(solution)/shard_map/k1/pallas_call | solution.py:347
  86.9 32.0 %k2.1 = (f32[4096,4352]{1,0:T(8,128)}, bf16[512,4352]{1,0:T(8,128)(2,1)}, bf16[2,32,4096]{2,1,0:T(8,128)(2,1)}, f32[64,4096]{1,0:T(8,128)}, f32[1,4096]{1,0:T(1,128)}) custom-call(bf16[512,4096]{1,0:T(8,128)(2,1)} %get-tuple-element.15.n_ref, bf16[512,4352]{1,0:T(8,128)(2,1)} %bitcast.5, bf16[512,4352]{1,0:T(8,128)(2,1)} %get-tuple-element.16.u_ref, ...), custom_call_target="tpu_custom_call" | custom-call | tf_op jit(solution)/shard_map/k2/pallas_call | solution.py:386

commit v4 on v3

v4 whole, which is shorter than its diff:
```python
import functools

import jax
import jax.numpy as jnp
from jax import lax
from jax.experimental import pallas as pl
from jax.experimental.pallas import tpu as pltpu
from jax.sharding import PartitionSpec as P

NORM_EPS = 1e-6
MESH = pl.DeviceIdType.MESH
F32 = jnp.float32
BF16 = jnp.bfloat16
FB = 512
NB = 8
UC = 512
TB = 128
DF = 256
RS = 4
WS = 3
CS = 3


def _flip(r, bits):
    for bit in (1, 2, 4):
        if bits & bit:
            r = r + bit - 2 * bit * (lax.rem(lax.div(r, bit), 2))
    return r


def _rcopy(src, dst, ssem, rsem, dev, dp=None):
    return pltpu.make_async_remote_copy(src_ref=src, dst_ref=dst, send_sem=ssem, recv_sem=rsem,
                                        device_id={"tp": dev} if dp is None else {"dp": dp, "tp": dev},
                                        device_id_type=MESH)


class _Gather:
    def __init__(self, r, chunk, ssem, rsem):
        self.r, self.chunk, self.ssem, self.rsem = r, chunk, ssem, rsem

    def send(self, rel_owner, h, to, idx):
        owner = _flip(self.r, rel_owner)
        return _rcopy(self.chunk(owner, h), self.chunk(owner, h), self.ssem.at[idx], self.rsem.at[2 * (rel_owner ^ to) + h],
                      _flip(self.r, to))

    def wait_in(self, rel_owner, h):
        owner = _flip(self.r, rel_owner)
        _rcopy(self.chunk(owner, h), self.chunk(owner, h), self.ssem.at[0], self.rsem.at[2 * rel_owner + h],
               _flip(self.r, 1)).wait_recv()

    def own(self):
        self.send(0, 0, 2, 0).start()
        self.send(0, 1, 4, 1).start()
        self.send(0, 1, 2, 2).start()
        self.send(0, 0, 4, 3).start()
        self.send(0, 0, 1, 4).start()
        self.send(0, 1, 1, 5).start()

    def fwd1(self):
        self.wait_in(2, 0)
        self.send(2, 0, 4, 6).start()
        self.send(2, 0, 1, 7).start()
        self.wait_in(4, 1)
        self.send(4, 1, 2, 8).start()
        self.send(4, 1, 1, 9).start()

    def fwd2(self):
        self.wait_in(2, 1)
        self.send(2, 1, 1, 10).start()
        self.wait_in(4, 0)
        self.send(4, 0, 1, 11).start()

    def fwd3(self):
        self.wait_in(6, 0)
        self.send(6, 0, 1, 12).start()
        self.wait_in(6, 1)
        self.send(6, 1, 1, 13).start()

    def finish(self):
        for rel in (1, 3, 5, 7):
            for h in (0, 1):
                self.wait_in(rel, h)
        for idx in range(14):
            self.send(0, 0, 1, idx).wait_send()


class _TableGather:
    def __init__(self, r, p, buf, tab, ssem, rsem):
        self.r, self.p, self.buf, self.tab, self.ssem, self.rsem = r, p, buf, tab, ssem, rsem

    def rows(self, k):
        return pl.ds(pl.multiple_of(16 * (k + self.p * (3 - 2 * k)), 16), 16)

    def own(self):
        for n, (to, k) in enumerate(((2, 0), (4, 2), (2, 1), (4, 3))):
            _rcopy(self.tab.at[self.rows(k)], self.buf.at[self.r, self.rows(k)], self.ssem.at[n],
                   self.rsem.at[2 * to + k], _flip(self.r, to)).start()
        _rcopy(self.tab, self.buf.at[self.r], self.ssem.at[4], self.rsem.at[0], _flip(self.r, 1)).start()

    def wait_in(self, rel, k):
        src = self.buf.at[_flip(self.r, rel), self.rows(k)]
        _rcopy(src, src, self.ssem.at[0], self.rsem.at[2 * rel + k], _flip(self.r, 1)).wait_recv()

    def fwd(self, rel, k, to, idx):
        src = self.buf.at[_flip(self.r, rel), self.rows(k)]
        _rcopy(src, src, self.ssem.at[idx], self.rsem.at[2 * (rel ^ to) + k], _flip(self.r, to)).start()

    def twin(self, rel, k, idx):
        src = self.buf.at[_flip(self.r, rel), self.rows(k)]
        _rcopy(src, src, self.ssem.at[idx], self.rsem.at[2 * rel + 3 - k], self.r, 1 - self.p).start()

    def block(self, rel, idx, start):
        src = self.buf.at[_flip(self.r, rel)]
        c = _rcopy(src, src, self.ssem.at[idx], self.rsem.at[rel // 2], _flip(self.r, 1))
        if start:
            c.start()
        else:
            c.wait_recv()

    def relay(self, n):
        for rel, k, to in ((2, n, 4), (4, 2 + n, 2)):
            self.wait_in(rel, k)
            self.fwd(rel, k, to, 5 + 2 * n + (rel // 4))
            self.twin(rel, k, 9 + 2 * n + (rel // 4))

    def blocks(self):
        for n, (rel, ks) in enumerate(((2, (2, 3)), (4, (0, 1)), (6, (0, 1, 2, 3)))):
            for k in ks:
                self.wait_in(rel, k)
            self.block(rel, 13 + n, True)

    def finish(self):
        _rcopy(self.tab, self.buf.at[self.r], self.ssem.at[4], self.rsem.at[0], _flip(self.r, 1)).wait_recv()
        for n, rel in enumerate((2, 4, 6)):
            self.block(rel, 13 + n, False)
        small = self.buf.at[self.r, self.rows(0)]
        for n in range(16):
            src = self.buf.at[self.r] if n in (4, 13, 14, 15) else small
            _rcopy(src, src, self.ssem.at[n], self.rsem.at[0], _flip(self.r, 1)).wait_send()


def _k1(ids, gain, tab, w, du, dres, u_out, x_out, n_out, de_out, dg_out,
        du_v, w_v, etab, dn_v, rx1, tx2, rx2, own, wc_v, u_v, n_v, nh_v, inv_v, x_v, dres_v, dx_all, dgs,
        lsem, wsem, wcsem, usem, e_s, e_r, s1, r1, s2, r2, a_s, a_r, g_s, g_r):
    r = lax.axis_index("tp")
    p = lax.axis_index("dp")
    core = lax.rem(r, 2)
    xs = lax.rem(lax.div(r, 2), 2)
    ys = lax.div(r, 4)
    cols = w.shape[1]
    n_u = cols // UC
    rest = cols - n_u * UC

    du_cp = pltpu.make_async_copy(du, du_v, lsem.at[0])
    du_cp.start()

    def w_cp(j, slot):
        return pltpu.make_async_copy(w.at[pl.ds(pl.multiple_of(j * FB, FB), FB)], w_v.at[slot], wsem.at[slot])

    def wc_cp(i, slot):
        return pltpu.make_async_copy(w.at[:, pl.ds(pl.multiple_of(i * UC, UC), UC)], wc_v.at[slot], wcsem.at[slot])

    def wr_cp():
        return pltpu.make_async_copy(w.at[:, pl.ds(n_u * UC, rest)], wc_v.at[n_u % CS, :, pl.ds(0, rest)],
                                     wcsem.at[n_u % CS])

    def ur_cp():
        return pltpu.make_async_copy(u_v.at[n_u % 2, :, pl.ds(0, rest)], u_out.at[:, pl.ds(n_u * UC, rest)],
                                     usem.at[n_u % 2])

    def u_cp(i, slot):
        return pltpu.make_async_copy(u_v.at[slot], u_out.at[:, pl.ds(pl.multiple_of(i * UC, UC), UC)], usem.at[slot])

    for k in range(WS - 1):
        w_cp(k, k).start()
    tab_cp = pltpu.make_async_copy(tab, etab.at[r], lsem.at[2])
    tab_cp.start()
    dres_cp = pltpu.make_async_copy(dres, dres_v, lsem.at[3])
    dres_cp.start()

    barrier = pltpu.get_barrier_semaphore()
    for rel in range(1, 8):
        pl.semaphore_signal(barrier, inc=1, device_id={"tp": _flip(r, rel)}, device_id_type=MESH)
    pl.semaphore_signal(barrier, inc=1, device_id={"dp": 1 - p, "tp": r}, device_id_type=MESH)
    pl.semaphore_wait(barrier, 8)

    eg = _TableGather(r, p, etab, tab, e_s, e_r)
    eg.own()
    du_cp.wait()

    def rs1(j, m, even):
        if even:
            sib = dn_v.at[j, m, :, xs, 1 - core]
            far = [dn_v.at[j, m, :, 1 - xs, c] for c in range(2)]
            dev = [(ys * 2 + 1 - xs) * 2 + c for c in range(2)]
        else:
            sib = dn_v.at[j, m, ys, :, 1 - core]
            far = [dn_v.at[j, m, 1 - ys, :, c] for c in range(2)]
            dev = [((1 - ys) * 2 + xs) * 2 + c for c in range(2)]
        out = [_rcopy(far[c], rx1.at[j, m, 1 + core], s1.at[j, m, 1 + c], r1.at[j, m, 1 + core], dev[c])
               for c in range(2)]
        out.append(_rcopy(sib, rx1.at[j, m, 0], s1.at[j, m, 0], r1.at[j, m, 0], _flip(r, 1)))
        return out

    def rs1_start(j, m):
        if isinstance(j, int):
            for c in rs1(j, m, j % 2 == 0):
                c.start()
            return

        @pl.when(lax.rem(j, 2) == 0)
        def _():
            for c in rs1(j, m, True):
                c.start()

        @pl.when(lax.rem(j, 2) == 1)
        def _():
            for c in rs1(j, m, False):
                c.start()

    def combine(m, pair):
        for j in (2 * pair, 2 * pair + 1):
            oy, ox, q = (1 - ys, xs, ys) if j % 2 == 0 else (ys, 1 - xs, xs)
            for n in range(3):
                _rcopy(rx1.at[j, m, n], rx1.at[j, m, n], s1.at[j, m, 0], r1.at[j, m, n], _flip(r, 1)).wait_recv()

            def total(part, qi):
                t = part.astype(F32)
                for n in range(3):
                    t = t + rx1[j, m, n, qi].astype(F32)
                return t

            tx2[m, j] = total(dn_v[j, m, oy, ox, core], 1 - q)
            own[m, j] = total(dn_v[j, m, ys, xs, core], q)

    def rs2(m, j):
        oy, ox = (1 - ys, xs) if j % 2 == 0 else (ys, 1 - xs)
        return _rcopy(tx2.at[m, j], rx2.at[m, j], s2.at[m, j], r2.at[m, j], (oy * 2 + ox) * 2 + core)

    def rs2_start(m, pair):
        rs2(m, 2 * pair).start()
        rs2(m, 2 * pair + 1).start()

    def dn_step(j, carry):
        slot = lax.rem(j, WS)
        w_cp(j, slot).wait()

        @pl.when(j + WS - 1 < NB)
        def _():
            w_cp(j + WS - 1, lax.rem(j + WS - 1, WS)).start()

        part = lax.dot_general(du_v[...], w_v[slot], (((1,), (1,)), ((), ())),
                               preferred_element_type=F32)
        dn_v[j] = part.astype(BF16).reshape(2, 2, 2, 2, 32, FB)

        for n in range(2):
            @pl.when(j == n)
            def _():
                eg.relay(n)

        @pl.when(j == 2)
        def _():
            rs1_start(0, 0)

        @pl.when(j > 1)
        def _():
            rs1_start(j - 1, 0)

        @pl.when(j > 3)
        def _():
            rs1_start(j - 4, 1)

        @pl.when(j == 4)
        def _():
            eg.blocks()

        @pl.when(j == NB - 2)
        def _():
            for k in range(CS - 1):
                wc_cp(k, k).start()

        return carry

    lax.fori_loop(0, NB, dn_step, 0)
    tab_cp.wait()
    rs1_start(7, 0)
    rs1_start(4, 1)
    combine(0, 0)
    combine(0, 1)
    eg.finish()

    gf = gain[...].astype(F32).reshape(1, 4096)

    def one_hot(first, rows, tok):
        return (tok == first + lax.broadcasted_iota(jnp.int32, (rows, tok.shape[1]), 0)).astype(BF16)

    def lookup(pick_t):
        return lax.dot_general(pick_t, etab[...].reshape(512, 4096), (((0,), (0,)), ((), ())),
                               preferred_element_type=F32)

    for b in range(512 // TB):
        rows = slice(b * TB, (b + 1) * TB)
        col = b * TB % 256
        xg = lookup(one_hot(0, 512, ids[b * TB // 256:b * TB // 256 + 1, col:col + TB]))
        inv = lax.rsqrt(jnp.mean(xg * xg, axis=-1, keepdims=True) + NORM_EPS)
        n_v[rows, :] = (xg * inv * gf).astype(BF16)
        if b == 0:
            rs2_start(0, 0)
            rs2_start(0, 1)

    n_cp = pltpu.make_async_copy(n_v, n_out, lsem.at[0])
    n_cp.start()

    mine = (lax.broadcasted_iota(jnp.int32, (32, 256), 1) ==
            r * 32 + lax.broadcasted_iota(jnp.int32, (32, 256), 0)).astype(BF16)
    pick_own = jnp.concatenate(
        [lax.dot_general(mine, one_hot(0, 512, ids[m:m + 1, :]), (((1,), (1,)), ((), ())), preferred_element_type=F32)
         for m in range(2)], axis=0).astype(BF16)
    xo = jnp.dot(pick_own, etab[...].reshape(512, 4096), preferred_element_type=F32)
    inv_own = lax.rsqrt(jnp.mean(xo * xo, axis=-1, keepdims=True) + NORM_EPS)
    x_v[...] = xo.astype(BF16).reshape(2, 32, 4096)
    nh_v[...] = xo * inv_own
    inv_v[...] = jnp.broadcast_to(inv_own, (64, 128))
    x_cp = pltpu.make_async_copy(x_v, x_out, lsem.at[1])
    x_cp.start()

    def dx_of(m):
        rows = slice(32 * m, 32 * m + 32)
        centre = jnp.zeros((32, 1), F32)
        for j in range(NB):
            sl = slice(j * FB, (j + 1) * FB)
            rs2(m, j).wait_recv()
            dn = own[m, j] + rx2[m, j]
            own[m, j] = dn
            nh = nh_v[rows, sl]
            centre = centre + jnp.sum(nh * (gf[:, sl] * dn), axis=-1, keepdims=True)
            part = jnp.sum(dn * nh, axis=0, keepdims=True)
            dgs[r, :, sl] = part if m == 0 else dgs[r, :, sl] + part
        centre = centre * (1.0 / 4096)
        for j in range(NB):
            sl = slice(j * FB, (j + 1) * FB)
            dr = dres_v[m, :, sl].astype(F32)
            dx = dr + inv_v[rows, 0:1] * (gf[:, sl] * own[m, j] - nh_v[rows, sl] * centre)
            dx_all[m, r, :, sl] = dx.astype(BF16)

    def dx_gather(m):
        return _Gather(r, lambda owner, h: dx_all.at[m, owner, pl.ds(16 * h, 16)], a_s.at[m], a_r.at[m])

    ag = [dx_gather(m) for m in range(2)]
    dres_cp.wait()
    combine(0, 2)
    events = {
        0: lambda: rs2_start(0, 2),
        1: lambda: (rs1_start(5, 1), combine(0, 3)),
        2: lambda: (rs2_start(0, 3), rs1_start(6, 1), rs1_start(7, 1), combine(1, 0)),
        3: lambda: (rs2_start(1, 0), combine(1, 1)),
        4: lambda: (rs2_start(1, 1), combine(1, 2)),
        5: lambda: (rs2_start(1, 2), dx_of(0)),
        6: lambda: (ag[0].own(), combine(1, 3)),
        7: lambda: rs2_start(1, 3),
    }

    def u_step(i, carry):
        slot = lax.rem(i, 2)
        wslot = lax.rem(i, CS)
        wc_cp(i, wslot).wait()

        @pl.when(i + CS - 1 < n_u)
        def _():
            wc_cp(i + CS - 1, lax.rem(i + CS - 1, CS)).start()

        @pl.when(i + CS - 1 == n_u)
        def _():
            wr_cp().start()

        @pl.when(i >= 2)
        def _():
            u_cp(i - 2, slot).wait()

        u_v[slot] = jnp.dot(n_v[...], wc_v[wslot], preferred_element_type=F32).astype(BF16)
        u_cp(i, slot).start()

        for at, event in events.items():
            pl.when(i == at)(lambda event=event: (event(), None)[1])

        return carry

    lax.fori_loop(0, n_u, u_step, 0)
    wr_cp().wait()
    u_cp(n_u - 2, n_u % 2).wait()
    u_v[n_u % 2, :, :rest] = jnp.dot(n_v[...], wc_v[n_u % CS, :, :rest], preferred_element_type=F32).astype(BF16)
    ur_cp().start()
    ag[0].fwd1()
    ag[0].fwd2()
    dx_of(1)
    def dg_cp(rel):
        return _rcopy(dgs.at[r], dgs.at[r], g_s.at[rel], g_r.at[r], _flip(r, rel))

    ag[1].own()
    for rel in range(1, 8):
        dg_cp(rel).start()
    ag[0].fwd3()
    ag[1].fwd1()
    u_cp(n_u - 1, (n_u - 1) % 2).wait()
    ur_cp().wait()
    ag[0].finish()
    ag[1].fwd2()
    ag[1].fwd3()
    for rel in range(1, 8):
        src = _flip(r, rel)
        _rcopy(dgs.at[src], dgs.at[src], g_s.at[rel], g_r.at[src], src).wait_recv()
    tot = dgs[0]
    for k in range(1, 8):
        tot = tot + dgs[k]
    dg_out[...] = tot
    pick = jnp.concatenate([one_hot(r * 64, 64, ids[m:m + 1, :]) for m in range(2)], axis=1)
    ag[1].finish()
    de_out[...] = jnp.dot(pick, dx_all[...].reshape(512, 4096), preferred_element_type=F32)

    for rel in range(1, 8):
        dg_cp(rel).wait_send()
    for m in range(2):
        for j in range(NB):
            for c in rs1(j, m, j % 2 == 0):
                c.wait_send()
            rs2(m, j).wait_send()
    n_cp.wait()
    x_cp.wait()


def _k2(n_in, du_in, u_in, x_in, de_in, dg_in, dw_out, u_out, x_out, de_out, dg_out,
        n_v, du_v, ring, u_v, x_v, de_v, dg_v, lsem, psem, qsem, osem):
    steps = n_in.shape[1] // DF
    half = 9 * 256
    cols = du_in.shape[1]
    parts = (pl.ds(0, half), pl.ds(half, cols - half))
    cp = pltpu.make_async_copy
    loads = [cp(n_in.at[:, pl.ds(0, DF)], n_v.at[:, pl.ds(0, DF)], lsem.at[0]),
             cp(du_in.at[:, parts[0]], du_v.at[:, parts[0]], lsem.at[1]),
             cp(du_in.at[:, parts[1]], du_v.at[:, parts[1]], lsem.at[2]),
             cp(n_in.at[:, pl.ds(DF, (steps - 1) * DF)], n_v.at[:, pl.ds(DF, (steps - 1) * DF)], lsem.at[3])]
    through = ((u_in, u_v, u_out), (x_in, x_v, x_out), (de_in, de_v, de_out), (dg_in, dg_v, dg_out))
    ins = [cp(a, b, psem.at[k]) for k, (a, b, _) in enumerate(through)]
    outs = [cp(b, c, qsem.at[k]) for k, (_, b, c) in enumerate(through)]
    for c in loads + ins:
        c.start()

    def store(i, slot):
        return cp(ring.at[slot], dw_out.at[pl.ds(pl.multiple_of(i * DF, DF), DF)], osem.at[slot])

    loads[0].wait()
    loads[1].wait()

    def step(i, carry):
        slot = lax.rem(i, RS)
        sl = pl.ds(pl.multiple_of(i * DF, DF), DF)

        @pl.when(i >= RS)
        def _():
            store(i - RS, slot).wait()

        @pl.when(i == 1)
        def _():
            loads[3].wait()

        for k, part in enumerate(parts):
            if k == 1:
                @pl.when(i == 0)
                def _():
                    loads[2].wait()
            ring[slot, :, part] = lax.dot_general(n_v[:, sl], du_v[:, part], (((0,), (0,)), ((), ())),
                                                  preferred_element_type=F32)
        store(i, slot).start()

        @pl.when(i == 2)
        def _():
            for a, b in zip(ins, outs):
                a.wait()
                b.start()

        return carry

    lax.fori_loop(0, steps, step, 0)
    for i in range(steps - RS, steps):
        store(i, i % RS).wait()
    for c in outs:
        c.wait()


def solution(mesh):
    group_size = mesh.shape['tp']

    def local_step(token_ids, table_loc, gain_vec, w_loc, du_loc, dres_loc):
        num_micro, seq_len = token_ids.shape
        rows_loc, model_dim = table_loc.shape
        seq_loc = seq_len // group_size
        cols_loc = w_loc.shape[1]
        tokens = num_micro * seq_len
        du_flat = du_loc.reshape(tokens, cols_loc)
        vm, hb = pl.BlockSpec(memory_space=pltpu.VMEM), pl.BlockSpec(memory_space=pl.ANY)
        sd = jax.ShapeDtypeStruct
        dma = pltpu.SemaphoreType.DMA
        u_all, x_own, normed, grad_table, grad_gain = pl.pallas_call(
            _k1,
            out_shape=(sd((tokens, cols_loc), BF16), sd((num_micro, seq_loc, model_dim), BF16),
                       sd((tokens, model_dim), BF16), sd((rows_loc, model_dim), F32), sd((1, model_dim), F32)),
            in_specs=[vm, vm, hb, hb, hb, hb],
            out_specs=(hb, hb, hb, vm, vm),
            scratch_shapes=[
                pltpu.VMEM((tokens, cols_loc), BF16),
                pltpu.VMEM((WS, FB, cols_loc), BF16),
                pltpu.VMEM((8, 64, model_dim), BF16),
                pltpu.VMEM((NB, 2, 2, 2, 2, 32, FB), BF16),
                pltpu.VMEM((NB, 2, 3, 2, 32, FB), BF16),
                pltpu.VMEM((2, NB, 32, FB), F32),
                pltpu.VMEM((2, NB, 32, FB), F32),
                pltpu.VMEM((2, NB, 32, FB), F32),
                pltpu.VMEM((CS, model_dim, UC), BF16),
                pltpu.VMEM((2, tokens, UC), BF16),
                pltpu.VMEM((tokens, model_dim), BF16),
                pltpu.VMEM((64, model_dim), F32),
                pltpu.VMEM((64, 128), F32),
                pltpu.VMEM((2, 32, model_dim), BF16),
                pltpu.VMEM((2, 32, model_dim), BF16),
                pltpu.VMEM((2, 8, 32, model_dim), BF16),
                pltpu.VMEM((8, 1, model_dim), F32),
                dma((4,)), dma((WS,)), dma((CS,)), dma((2,)),
                dma((16,)), dma((16,)),
                dma((NB, 2, 3)), dma((NB, 2, 3)), dma((2, NB)), dma((2, NB)),
                dma((2, 14)), dma((2, 16)),
                dma((8,)), dma((8,)),
            ],
            compiler_params=pltpu.CompilerParams(collective_id=0, has_side_effects=True,
                                                 vmem_limit_bytes=67043328),
            name="k1",
        )(token_ids, gain_vec, table_loc, w_loc,
          du_flat, dres_loc)
        grad_w, u_all, x_own, grad_table, grad_gain = pl.pallas_call(
            _k2,
            out_shape=(sd((model_dim, cols_loc), F32), sd((tokens, cols_loc), BF16),
                       sd((num_micro, seq_loc, model_dim), BF16), sd((rows_loc, model_dim), F32),
                       sd((1, model_dim), F32)),
            in_specs=[hb] * 6,
            out_specs=(hb,) * 5,
            scratch_shapes=[
                pltpu.VMEM((tokens, model_dim), BF16), pltpu.VMEM((tokens, cols_loc), BF16),
                pltpu.VMEM((RS, DF, cols_loc), F32),
                pltpu.VMEM((tokens, cols_loc), BF16), pltpu.VMEM((num_micro, seq_loc, model_dim), BF16),
                pltpu.VMEM((rows_loc, model_dim), F32), pltpu.VMEM((1, model_dim), F32),
                dma((4,)), dma((4,)), dma((4,)), dma((RS,)),
            ],
            compiler_params=pltpu.CompilerParams(vmem_limit_bytes=60 * 2 ** 20),
            name="k2",
        )(normed, du_flat, u_all, x_own, grad_table, grad_gain)
        return u_all.reshape(num_micro, seq_len, cols_loc), x_own, grad_table, grad_w, grad_gain.reshape(model_dim)

    return jax.shard_map(local_step, mesh=mesh,
                         in_specs=(P('dp', None), P('tp', None), P(None), P(None, 'tp'), P('dp', None, 'tp'), P('dp', 'tp', None)),
                         out_specs=(P('dp', None, 'tp'), P('dp', 'tp', None), P(('dp', 'tp'), None), P(None, ('dp', 'tp')), P('dp')),
                         check_vma=False)
```

time: 119 us -> 112 us (0.941)
  Pallas kernels: 118 us -> 111 us
    pallas_call x1, Pallas kernels: 86.3 us -> 79.8 us  [local_step(): pl.pallas_call(_k1, out_shape=(sd((tokens, cols_loc), BF16), sd((num_micr...]
where the time goes in v4:
time: 112 us
  Pallas kernels  111 us (99%)
    pallas_call x1, Pallas kernels, local_step(): pl.pallas_call(_k1, out_shape=(sd((tokens, cols_loc), BF16), sd((num_micr...  79.8 us
    pallas_call x1, Pallas kernels, local_step(): pl.pallas_call(_k2, out_shape=(sd((model_dim, cols_loc), F32), sd((tokens...  31.5 us

profile of v4, /device:TPU:0, one launch (start us, length us, event | category | flops | bytes accessed | tf_op | source)
XLA Modules:
  0.0 111.9 jit_solution(7341833313130887663)
XLA Ops:
  0.6 79.8 %k1.1 = (bf16[512,4352]{1,0:T(8,128)(2,1)}, bf16[2,32,4096]{2,1,0:T(8,128)(2,1)}, bf16[512,4096]{1,0:T(8,128)(2,1)}, f32[64,4096]{1,0:T(8,128)}, f32[1,4096]{1,0:T(1,128)}) custom-call(s32[2,256]{1,0:T(2,128)} %ids.1, bf16[4096]{0:T(1024)(128)(2,1)} %gain.1, bf16[64,4096]{1,0:T(8,128)(2,1)} %tab.1, bf16[4096,4352]{1,0:T(8,128)(2,1)} %w.1, ...), custom_call_target="tpu_custom_call" | custom-call | tf_op jit(solution)/shard_map/k1/pallas_call | solution.py:503
  80.4 31.5 %k2.1 = (f32[4096,4352]{1,0:T(8,128)}, bf16[512,4352]{1,0:T(8,128)(2,1)}, bf16[2,32,4096]{2,1,0:T(8,128)(2,1)}, f32[64,4096]{1,0:T(8,128)}, f32[1,4096]{1,0:T(1,128)}) custom-call(bf16[512,4096]{1,0:T(8,128)(2,1)} %get-tuple-element.15.n_in, bf16[512,4352]{1,0:T(8,128)(2,1)} %bitcast.4, bf16[512,4352]{1,0:T(8,128)(2,1)} %get-tuple-element.16.u_in, ...), custom_call_target="tpu_custom_call" | custom-call | tf_op jit(solution)/shard_map/k2/pallas_call | solution.py:538

commit v5 on v4

--- a/solution.py
+++ b/solution.py
@@ -13,12 +13,12 @@
 BF16 = jnp.bfloat16
 FB = 512
 NB = 8
-UC = 512
+UC = 256
 TB = 128
 DF = 256
 RS = 4
 WS = 3
-CS = 3
+CS = 4
 
 
 def _flip(r, bits):
@@ -149,7 +149,6 @@
     ys = lax.div(r, 4)
     cols = w.shape[1]
     n_u = cols // UC
-    rest = cols - n_u * UC
 
     du_cp = pltpu.make_async_copy(du, du_v, lsem.at[0])
     du_cp.start()
@@ -159,14 +158,6 @@
 
     def wc_cp(i, slot):
         return pltpu.make_async_copy(w.at[:, pl.ds(pl.multiple_of(i * UC, UC), UC)], wc_v.at[slot], wcsem.at[slot])
-
-    def wr_cp():
-        return pltpu.make_async_copy(w.at[:, pl.ds(n_u * UC, rest)], wc_v.at[n_u % CS, :, pl.ds(0, rest)],
-                                     wcsem.at[n_u % CS])
-
-    def ur_cp():
-        return pltpu.make_async_copy(u_v.at[n_u % 2, :, pl.ds(0, rest)], u_out.at[:, pl.ds(n_u * UC, rest)],
-                                     usem.at[n_u % 2])
 
     def u_cp(i, slot):
         return pltpu.make_async_copy(u_v.at[slot], u_out.at[:, pl.ds(pl.multiple_of(i * UC, UC), UC)], usem.at[slot])
@@ -270,9 +261,18 @@
         def _():
             rs1_start(j - 4, 1)
 
-        @pl.when(j == 4)
+        @pl.when(j == 5)
         def _():
             eg.blocks()
+
+        @pl.when(j == 6)
+        def _():
+            combine(0, 0)
+
+        @pl.when(j == 7)
+        def _():
+            rs2_start(0, 0)
+            combine(0, 1)
 
         @pl.when(j == NB - 2)
         def _():
@@ -284,9 +284,9 @@
     lax.fori_loop(0, NB, dn_step, 0)
     tab_cp.wait()
     rs1_start(7, 0)
+    rs2_start(0, 1)
     rs1_start(4, 1)
-    combine(0, 0)
-    combine(0, 1)
+    rs1_start(5, 1)
     eg.finish()
 
     gf = gain[...].astype(F32).reshape(1, 4096)
@@ -304,9 +304,6 @@
         xg = lookup(one_hot(0, 512, ids[b * TB // 256:b * TB // 256 + 1, col:col + TB]))
         inv = lax.rsqrt(jnp.mean(xg * xg, axis=-1, keepdims=True) + NORM_EPS)
         n_v[rows, :] = (xg * inv * gf).astype(BF16)
-        if b == 0:
-            rs2_start(0, 0)
-            rs2_start(0, 1)
 
     n_cp = pltpu.make_async_copy(n_v, n_out, lsem.at[0])
     n_cp.start()
@@ -348,16 +345,20 @@
 
     ag = [dx_gather(m) for m in range(2)]
     dres_cp.wait()
-    combine(0, 2)
     events = {
-        0: lambda: rs2_start(0, 2),
-        1: lambda: (rs1_start(5, 1), combine(0, 3)),
-        2: lambda: (rs2_start(0, 3), rs1_start(6, 1), rs1_start(7, 1), combine(1, 0)),
-        3: lambda: (rs2_start(1, 0), combine(1, 1)),
-        4: lambda: (rs2_start(1, 1), combine(1, 2)),
-        5: lambda: (rs2_start(1, 2), dx_of(0)),
-        6: lambda: (ag[0].own(), combine(1, 3)),
-        7: lambda: rs2_start(1, 3),
+        0: lambda: (combine(0, 2),),
+        1: lambda: (rs2_start(0, 2), combine(0, 3),),
+        2: lambda: (rs2_start(0, 3), rs1_start(6, 1), rs1_start(7, 1), combine(1, 0),),
+        3: lambda: (rs2_start(1, 0), combine(1, 1),),
+        4: lambda: (rs2_start(1, 1), combine(1, 2),),
+        5: lambda: (rs2_start(1, 2), dx_of(0),),
+        6: lambda: (combine(1, 3),),
+        7: lambda: (rs2_start(1, 3), ag[0].own(),),
+        9: lambda: (dx_of(1),),
+        10: lambda: (ag[1].own(),),
+        11: lambda: (ag[0].fwd1(),),
+        13: lambda: (ag[0].fwd2(),),
+        15: lambda: (ag[1].fwd1(),),
     }
 
     def u_step(i, carry):
@@ -369,10 +370,6 @@
         def _():
             wc_cp(i + CS - 1, lax.rem(i + CS - 1, CS)).start()
 
-        @pl.when(i + CS - 1 == n_u)
-        def _():
-            wr_cp().start()
-
         @pl.when(i >= 2)
         def _():
             u_cp(i - 2, slot).wait()
@@ -386,25 +383,21 @@
         return carry
 
     lax.fori_loop(0, n_u, u_step, 0)
-    wr_cp().wait()
-    u_cp(n_u - 2, n_u % 2).wait()
-    u_v[n_u % 2, :, :rest] = jnp.dot(n_v[...], wc_v[n_u % CS, :, :rest], preferred_element_type=F32).astype(BF16)
-    ur_cp().start()
-    ag[0].fwd1()
-    ag[0].fwd2()
-    dx_of(1)
     def dg_cp(rel):
         return _rcopy(dgs.at[r], dgs.at[r], g_s.at[rel], g_r.at[r], _flip(r, rel))
 
-    ag[1].own()
     for rel in range(1, 8):
         dg_cp(rel).start()
     ag[0].fwd3()
-    ag[1].fwd1()
+    u_cp(n_u - 2, n_u % 2).wait()
     u_cp(n_u - 1, (n_u - 1) % 2).wait()
-    ur_cp().wait()
     ag[0].finish()
     ag[1].fwd2()
+
+    def grad_rows(m):
+        return jnp.dot(one_hot(r * 64, 64, ids[m:m + 1, :]), dx_all[m].reshape(256, 4096), preferred_element_type=F32)
+
+    de = grad_rows(0)
     ag[1].fwd3()
     for rel in range(1, 8):
         src = _flip(r, rel)
@@ -413,9 +406,8 @@
     for k in range(1, 8):
         tot = tot + dgs[k]
     dg_out[...] = tot
-    pick = jnp.concatenate([one_hot(r * 64, 64, ids[m:m + 1, :]) for m in range(2)], axis=1)
     ag[1].finish()
-    de_out[...] = jnp.dot(pick, dx_all[...].reshape(512, 4096), preferred_element_type=F32)
+    de_out[...] = de + grad_rows(1)
 
     for rel in range(1, 8):
         dg_cp(rel).wait_send()

time: 112 us -> 108 us (0.964)
  Pallas kernels: 111 us -> 107 us
    pallas_call x1, Pallas kernels: 79.8 us -> 75.7 us  [local_step(): pl.pallas_call(_k1, out_shape=(sd((tokens, cols_loc), BF16), sd((num_micr...]
where the time goes in v5:
time: 108 us
  Pallas kernels  107 us (99%)
    pallas_call x1, Pallas kernels, local_step(): pl.pallas_call(_k1, out_shape=(sd((tokens, cols_loc), BF16), sd((num_micr...  75.7 us
    pallas_call x1, Pallas kernels, local_step(): pl.pallas_call(_k2, out_shape=(sd((model_dim, cols_loc), F32), sd((tokens...  31.5 us

profile of v5, /device:TPU:0, one launch (start us, length us, event | category | flops | bytes accessed | tf_op | source)
XLA Modules:
  0.0 107.8 jit_solution(16618003590487051392)
XLA Ops:
  0.6 75.7 %k1.1 = (bf16[512,4352]{1,0:T(8,128)(2,1)}, bf16[2,32,4096]{2,1,0:T(8,128)(2,1)}, bf16[512,4096]{1,0:T(8,128)(2,1)}, f32[64,4096]{1,0:T(8,128)}, f32[1,4096]{1,0:T(1,128)}) custom-call(s32[2,256]{1,0:T(2,128)} %ids.1, bf16[4096]{0:T(1024)(128)(2,1)} %gain.1, bf16[64,4096]{1,0:T(8,128)(2,1)} %tab.1, bf16[4096,4352]{1,0:T(8,128)(2,1)} %w.1, ...), custom_call_target="tpu_custom_call" | custom-call | tf_op jit(solution)/shard_map/k1/pallas_call | solution.py:495
  76.3 31.5 %k2.1 = (f32[4096,4352]{1,0:T(8,128)}, bf16[512,4352]{1,0:T(8,128)(2,1)}, bf16[2,32,4096]{2,1,0:T(8,128)(2,1)}, f32[64,4096]{1,0:T(8,128)}, f32[1,4096]{1,0:T(1,128)}) custom-call(bf16[512,4096]{1,0:T(8,128)(2,1)} %get-tuple-element.15.n_in, bf16[512,4352]{1,0:T(8,128)(2,1)} %bitcast.4, bf16[512,4352]{1,0:T(8,128)(2,1)} %get-tuple-element.16.u_in, ...), custom_call_target="tpu_custom_call" | custom-call | tf_op jit(solution)/shard_map/k2/pallas_call | solution.py:530

commit v6 on v5

--- a/solution.py
+++ b/solution.py
@@ -455,13 +455,11 @@
         def _():
             loads[3].wait()
 
-        for k, part in enumerate(parts):
-            if k == 1:
-                @pl.when(i == 0)
-                def _():
-                    loads[2].wait()
-            ring[slot, :, part] = lax.dot_general(n_v[:, sl], du_v[:, part], (((0,), (0,)), ((), ())),
-                                                  preferred_element_type=F32)
+        @pl.when(i == 0)
+        def _():
+            loads[2].wait()
+
+        ring[slot] = lax.dot_general(n_v[:, sl], du_v[...], (((0,), (0,)), ((), ())), preferred_element_type=F32)
         store(i, slot).start()
 
         @pl.when(i == 2)

time: 108 us -> 106 us (0.981)
  Pallas kernels: 107 us -> 105 us
    pallas_call x1, Pallas kernels: 31.5 us -> 29.5 us  [local_step(): pl.pallas_call(_k2, out_shape=(sd((model_dim, cols_loc), F32), sd((tokens...]
where the time goes in v6:
time: 106 us
  Pallas kernels  105 us (99%)
    pallas_call x1, Pallas kernels, local_step(): pl.pallas_call(_k1, out_shape=(sd((tokens, cols_loc), BF16), sd((num_micr...  75.7 us
    pallas_call x1, Pallas kernels, local_step(): pl.pallas_call(_k2, out_shape=(sd((model_dim, cols_loc), F32), sd((tokens...  29.5 us

profile of v6, /device:TPU:0, one launch (start us, length us, event | category | flops | bytes accessed | tf_op | source)
XLA Modules:
  0.0 105.9 jit_solution(5143085907148770355)
XLA Ops:
  0.6 75.7 %k1.1 = (bf16[512,4352]{1,0:T(8,128)(2,1)}, bf16[2,32,4096]{2,1,0:T(8,128)(2,1)}, bf16[512,4096]{1,0:T(8,128)(2,1)}, f32[64,4096]{1,0:T(8,128)}, f32[1,4096]{1,0:T(1,128)}) custom-call(s32[2,256]{1,0:T(2,128)} %ids.1, bf16[4096]{0:T(1024)(128)(2,1)} %gain.1, bf16[64,4096]{1,0:T(8,128)(2,1)} %tab.1, bf16[4096,4352]{1,0:T(8,128)(2,1)} %w.1, ...), custom_call_target="tpu_custom_call" | custom-call | tf_op jit(solution)/shard_map/k1/pallas_call | solution.py:493
  76.3 29.5 %k2.1 = (f32[4096,4352]{1,0:T(8,128)}, bf16[512,4352]{1,0:T(8,128)(2,1)}, bf16[2,32,4096]{2,1,0:T(8,128)(2,1)}, f32[64,4096]{1,0:T(8,128)}, f32[1,4096]{1,0:T(1,128)}) custom-call(bf16[512,4096]{1,0:T(8,128)(2,1)} %get-tuple-element.15.n_in, bf16[512,4352]{1,0:T(8,128)(2,1)} %bitcast.4, bf16[512,4352]{1,0:T(8,128)(2,1)} %get-tuple-element.16.u_in, ...), custom_call_target="tpu_custom_call" | custom-call | tf_op jit(solution)/shard_map/k2/pallas_call | solution.py:528

commit v7 on v6

--- a/solution.py
+++ b/solution.py
@@ -120,14 +120,25 @@
     def relay(self, n):
         for rel, k, to in ((2, n, 4), (4, 2 + n, 2)):
             self.wait_in(rel, k)
-            self.fwd(rel, k, to, 5 + 2 * n + (rel // 4))
+            if n == 0:
+                self.fwd(rel, k, to, 5 + rel // 4)
             self.twin(rel, k, 9 + 2 * n + (rel // 4))
 
+    def diagonal(self):
+        for n, k in enumerate((0, 2)):
+            self.wait_in(6, k)
+            self.twin(6, k, 7 + n)
+
     def blocks(self):
-        for n, (rel, ks) in enumerate(((2, (2, 3)), (4, (0, 1)), (6, (0, 1, 2, 3)))):
+        for n, (rel, ks) in enumerate(((2, (2, 3)), (4, (0, 1)))):
             for k in ks:
                 self.wait_in(rel, k)
             self.block(rel, 13 + n, True)
+
+    def last_block(self):
+        for k in (1, 3):
+            self.wait_in(6, k)
+        self.block(6, 15, True)
 
     def finish(self):
         _rcopy(self.tab, self.buf.at[self.r], self.ssem.at[4], self.rsem.at[0], _flip(self.r, 1)).wait_recv()
@@ -249,11 +260,7 @@
             def _():
                 eg.relay(n)
 
-        @pl.when(j == 2)
-        def _():
-            rs1_start(0, 0)
-
-        @pl.when(j > 1)
+        @pl.when(j > 0)
         def _():
             rs1_start(j - 1, 0)
 
@@ -261,7 +268,11 @@
         def _():
             rs1_start(j - 4, 1)
 
-        @pl.when(j == 5)
+        @pl.when(j == 3)
+        def _():
+            eg.diagonal()
+
+        @pl.when(j == 7)
         def _():
             eg.blocks()
 
@@ -287,6 +298,7 @@
     rs2_start(0, 1)
     rs1_start(4, 1)
     rs1_start(5, 1)
+    eg.last_block()
     eg.finish()
 
     gf = gain[...].astype(F32).reshape(1, 4096)

time: 106 us -> 106 us (level)
  no operation moved by 1% of the time
where the time goes in v7:
time: 106 us
  Pallas kernels  105 us (99%)
    pallas_call x1, Pallas kernels, local_step(): pl.pallas_call(_k1, out_shape=(sd((tokens, cols_loc), BF16), sd((num_micr...  75.5 us
    pallas_call x1, Pallas kernels, local_step(): pl.pallas_call(_k2, out_shape=(sd((model_dim, cols_loc), F32), sd((tokens...  29.5 us

profile of v7, /device:TPU:0, one launch (start us, length us, event | category | flops | bytes accessed | tf_op | source)
XLA Modules:
  0.0 105.7 jit_solution(1311886649045145941)
XLA Ops:
  0.6 75.5 %k1.1 = (bf16[512,4352]{1,0:T(8,128)(2,1)}, bf16[2,32,4096]{2,1,0:T(8,128)(2,1)}, bf16[512,4096]{1,0:T(8,128)(2,1)}, f32[64,4096]{1,0:T(8,128)}, f32[1,4096]{1,0:T(1,128)}) custom-call(s32[2,256]{1,0:T(2,128)} %ids.1, bf16[4096]{0:T(1024)(128)(2,1)} %gain.1, bf16[64,4096]{1,0:T(8,128)(2,1)} %tab.1, bf16[4096,4352]{1,0:T(8,128)(2,1)} %w.1, ...), custom_call_target="tpu_custom_call" | custom-call | tf_op jit(solution)/shard_map/k1/pallas_call | solution.py:505
  76.2 29.5 %k2.1 = (f32[4096,4352]{1,0:T(8,128)}, bf16[512,4352]{1,0:T(8,128)(2,1)}, bf16[2,32,4096]{2,1,0:T(8,128)(2,1)}, f32[64,4096]{1,0:T(8,128)}, f32[1,4096]{1,0:T(1,128)}) custom-call(bf16[512,4096]{1,0:T(8,128)(2,1)} %get-tuple-element.15.n_in, bf16[512,4352]{1,0:T(8,128)(2,1)} %bitcast.4, bf16[512,4352]{1,0:T(8,128)(2,1)} %get-tuple-element.16.u_in, ...), custom_call_target="tpu_custom_call" | custom-call | tf_op jit(solution)/shard_map/k2/pallas_call | solution.py:540
